TPU v7x, 512 devices: a whole 4x4x16 slice. The times are simulated.
512 devices in a mesh: gx: 32 (over z, core), gy: 16 (over x, y).
Axes of the slice: x: 4, y: 4, z: 16, core: 2. Of those that a mesh axis runs over, the one named last changes fastest.
Arguments:
- blocks: bfloat16 [32, 16, 3, 320, 2240], P('gx', 'gy'), may hold values from -1 to 2
- right_side: bfloat16 [32, 16, 3, 320, 128], P('gx', 'gy'), may hold values from -6 to 6
- departure: int32 [32, 16, 2], P('gx', 'gy'), may hold values from -1 to 2, as said below
- arrival: int32 [32, 16, 2], P('gx', 'gy'), may hold values from 0 to 4, as said below
- neighbors: int32 [32, 16, 2, 6], P('gx', 'gy'), may hold values from 0 to 5, as said below
- orientation: int32 [32, 16, 2, 6], P('gx', 'gy'), may hold values from 0 to 3
Outputs:
- smoothed: float32 [32, 16, 2, 320, 128], P('gx', 'gy')
Inputs may be any that keep to these rules, and one draw needn't show every extreme that they name: Position (l, c) holds its rows in some of its 3 slots; its live slots are exactly those named in its departure or arrival entries, each once. At most one of the two entries is a slot; the device with c = 0 never sends lower, the one with c = 15 never upper. Every position holds 1 to 3 rows before and exactly 2 after; in every layer some position holds 3. `arrival`: values below 3 name a local slot, kept in rising order; 3 is the row that the lower gy neighbour sends upward, 4 the one the upper neighbour sends downward, consistent with departure. `neighbors`: face 0 names 0 or 1, face 1 names 4 or 5; no entry of row q names 2 + q.
All inputs are finite; a program needn't handle non-finite values.
Results may differ from a plain program's by a relative error of at most 0.0035.
Values may be sent and summed in bfloat16 or wider, within the bound.
No kernel may reach another device: no remote copies, remote signals or barrier semaphores. Data moves between devices by JAX's collectives and lax.ppermute only.
A program may use at most 64 MiB of HBM per device.

v0:
```python
import jax
import jax.numpy as jnp
from jax import lax
from jax.sharding import PartitionSpec as P

NODES = 4
ITERS = 4


RELAXATION = 0.7


def with_halo(block, sides, width):
    for axis, dim in sides:
        count = lax.axis_size(axis)
        forward = [(i, i + 1) for i in range(count - 1)]
        backward = [(target, source) for source, target in forward]
        low = lax.ppermute(
            lax.slice_in_dim(block, block.shape[dim] - width, None, axis=dim), axis, forward
        )
        high = lax.ppermute(lax.slice_in_dim(block, 0, width, axis=dim), axis, backward)
        block = jnp.concatenate([low, block, high], axis=dim)
    return block


def from_behind(value, axis, steps):
    count = lax.axis_size(axis)
    leading, last = (max(0, -steps), min(count, count - steps))
    return lax.ppermute(value, axis, [(source, source + steps) for source in range(leading, last)])


def turned_faces(faces, face_codes):
    row_count, face_count, dof_width, rhs_width = faces.shape
    nodal = faces.reshape(
        row_count, face_count, dof_width // NODES**3, NODES, NODES, NODES, rhs_width
    )
    result = nodal
    for quarter in range(1, 4):
        result = jnp.where(
            (face_codes == quarter)[:, :, None, None, None, None, None],
            jnp.rot90(nodal, quarter, axes=(3, 4)),
            result,
        )
    return result.reshape(row_count, face_count, dof_width, rhs_width)


def coupled(row_blocks, window, face_links, face_codes, own_rows):
    faces = turned_faces(jnp.take(window, face_links, axis=0), face_codes)
    stacked = jnp.concatenate([own_rows[:, None], faces], axis=1)
    stacked = stacked.reshape(stacked.shape[0], -1, stacked.shape[-1])
    return jnp.einsum("nde,ner->ndr", row_blocks, stacked, preferred_element_type=jnp.float32)


def layer_window(rounded):
    lifted = with_halo(rounded[None], (("gx", 0),), 1)
    return lifted.reshape(-1, rounded.shape[1], rounded.shape[2])


def shards(blocks, right_side, departure, arrival, neighbors, orientation):
    local_blocks = blocks[0, 0]
    local_rhs = right_side[0, 0]
    leaving_slots = departure[0, 0]
    sources = arrival[0, 0]
    face_links = neighbors[0, 0]
    face_codes = orientation[0, 0]
    lower_slot = jnp.maximum(leaving_slots[0], 0)
    upper_slot = jnp.maximum(leaving_slots[1], 0)
    from_upper = from_behind((local_blocks[lower_slot], local_rhs[lower_slot]), "gy", -1)
    from_lower = from_behind((local_blocks[upper_slot], local_rhs[upper_slot]), "gy", 1)
    block_pool = jnp.concatenate([local_blocks, from_lower[0][None], from_upper[0][None]], axis=0)
    rhs_pool = jnp.concatenate([local_rhs, from_lower[1][None], from_upper[1][None]], axis=0)
    kept_blocks = jnp.take(block_pool, sources, axis=0)
    kept_rhs = jnp.take(rhs_pool, sources, axis=0).astype(jnp.float32)
    current = RELAXATION * kept_rhs
    for sweep_index in range(ITERS):
        rounded = current.astype(jnp.bfloat16)
        window = layer_window(rounded)
        applied = coupled(kept_blocks, window, face_links, face_codes, rounded)
        current = current + RELAXATION * (kept_rhs - applied)
    return current[None, None]


def solution(mesh):
    in_specs = (
        P("gx", "gy", None, None, None),
        P("gx", "gy", None, None, None),
        P("gx", "gy", None),
        P("gx", "gy", None),
        P("gx", "gy", None, None),
        P("gx", "gy", None, None),
    )
    out_specs = P("gx", "gy", None, None, None)
    return jax.shard_map(shards, mesh=mesh, in_specs=in_specs, out_specs=out_specs, check_vma=False)
```

profile of v0, /device:TPU:410, one launch (start us, length us, event | category | flops | bytes accessed | tf_op | source)
XLA Modules:
  0.0 111.5 jit_solution(17694408059146228321)
XLA Ops:
  0.0 1.3 %fusion.19 = (s32[1,1,1]{2,1,0:T(1,128)}, s32[1,1,1]{2,1,0:T(1,128)}) fusion(s32[1,1,2]{2,1,0:T(1,128)} %param.10), kind=kLoop, calls=%fused_computation.77 | loop fusion | bytes 16 | tf_op jit(solution)/shard_map/slice | solution.py:67
  2.5 1.0 dynamic-slice_bitcast_fusion.3
  3.5 3.0 %collective-permute-start = (bf16[320,128]{1,0:T(8,128)(2,1)S(1)}, bf16[320,128]{1,0:T(8,128)(2,1)S(1)}, u32[]{:S(2)}, u32[]{:S(2)}) collective-permute-start(bf16[320,128]{1,0:T(8,128)(2,1)S(1)} %get-tuple-element.22), channel_id=1, source_target_pairs={{0,1},{1,2},{2,3},{3,4},{4,5},{5,6},{6,7},{7,8},{8,9},{9,10},{10,1... | collective-permute-start | bytes 245768 | tf_op jit(solution)/shard_map/ppermute | solution.py:29
  6.6 3.0 %collective-permute-start.1 = (bf16[320,128]{1,0:T(8,128)(2,1)S(1)}, bf16[320,128]{1,0:T(8,128)(2,1)S(1)}, u32[]{:S(2)}, u32[]{:S(2)}) collective-permute-start(bf16[320,128]{1,0:T(8,128)(2,1)S(1)} %get-tuple-element.23), channel_id=1, source_target_pairs={{1,0},{2,1},{3,2},{4,3},{5,4},{6,5},{7,6},{8,7},{9,8},{10,9},{11,1... | collective-permute-start | bytes 245768 | tf_op jit(solution)/shard_map/ppermute | solution.py:29
  9.6 3.7 %dynamic-slice_bitcast_fusion.1 = (bf16[320,2240]{1,0:T(8,128)(2,1)}, bf16[320,2240]{1,0:T(8,128)(2,1)}) fusion(bf16[1,1,3,320,2240]{4,3,2,1,0:T(8,128)(2,1)} %param.8, s32[]{:T(128)} %bitcast.2, s32[]{:T(128)} %bitcast.5), kind=kLoop, calls=%fused_computation.9 | loop fusion | bytes 5734408 | tf_op jit(solution)/shard_map/squeeze | solution.py:69
  13.2 5.1 %collective-permute-start.2 = (bf16[320,2240]{1,0:T(8,128)(2,1)}, bf16[320,2240]{1,0:T(8,128)(2,1)S(1)}, u32[]{:S(2)}, u32[]{:S(2)}) collective-permute-start(bf16[320,2240]{1,0:T(8,128)(2,1)} %get-tuple-element.6), channel_id=1, source_target_pairs={{0,1},{1,2},{2,3},{3,4},{4,5},{5,6},{6,7},{7,8},{8,9},{9,10},{10,1... | collective-permute-start | bytes 4300808 | tf_op jit(solution)/shard_map/ppermute | solution.py:29
  18.3 1.9 %collective-permute-start.3 = (bf16[320,2240]{1,0:T(8,128)(2,1)}, bf16[320,2240]{1,0:T(8,128)(2,1)}, u32[]{:S(2)}, u32[]{:S(2)}) collective-permute-start(bf16[320,2240]{1,0:T(8,128)(2,1)} %get-tuple-element.7), channel_id=1, source_target_pairs={{1,0},{2,1},{3,2},{4,3},{5,4},{6,5},{7,6},{8,7},{9,8},{10,9},{11,1... | collective-permute-start | bytes 4300808 | tf_op jit(solution)/shard_map/ppermute | solution.py:29
  20.3 0.1 reshape.228
  20.4 0.1 pad_maximum_fusion.9
  20.5 0.6 gather_fusion
  21.1 0.1 multiply_convert_fusion
  21.2 2.8 %collective-permute-start.5 = (bf16[1,2,320,128]{3,2,1,0:T(8,128)(2,1)S(1)}, bf16[1,2,320,128]{3,2,1,0:T(8,128)(2,1)S(1)}, u32[]{:S(2)}, u32[]{:S(2)}) collective-permute-start(bf16[1,2,320,128]{3,2,1,0:T(8,128)(2,1)S(1)} %multiply_convert_fusion), channel_id=1, source_target_pairs={{16,0},{32,16},{48,32},{64,48},{80,64},{96,80},{112,96},{128,112},... | collective-permute-start | bytes 491528 | tf_op jit(solution)/shard_map/ppermute | solution.py:21
  24.0 1.9 %collective-permute-start.4 = (bf16[1,2,320,128]{3,2,1,0:T(8,128)(2,1)S(1)}, bf16[1,2,320,128]{3,2,1,0:T(8,128)(2,1)S(1)}, u32[]{:S(2)}, u32[]{:S(2)}) collective-permute-start(bf16[1,2,320,128]{3,2,1,0:T(8,128)(2,1)S(1)} %multiply_convert_fusion), channel_id=1, source_target_pairs={{0,16},{16,32},{32,48},{48,64},{64,80},{80,96},{96,112},{112,128},... | collective-permute-start | bytes 491528 | tf_op jit(solution)/shard_map/ppermute | solution.py:18
  26.0 0.1 fusion.17
  26.1 0.8 collective-permute-done.5
  26.8 5.0 %collective-permute-done.4 = bf16[1,2,320,128]{3,2,1,0:T(8,128)(2,1)S(1)} collective-permute-done((bf16[1,2,320,128]{3,2,1,0:T(8,128)(2,1)S(1)}, bf16[1,2,320,128]{3,2,1,0:T(8,128)(2,1)S(1)}, u32[]{:S(2)}, u32[]{:S(2)}) %collective-permute-start.4) | collective-permute-done | bytes 163872 | tf_op jit(solution)/shard_map/ppermute | solution.py:18
  31.9 0.1 pad_maximum_fusion.5
  31.9 0.7 gather_fusion.2
  32.7 0.2 broadcast_select_fusion.4
  32.9 0.4 copy.58
  33.3 1.4 %fusion.16 = bf16[2,6,5,4,4,4,128]{6,5,4,3,2,1,0:T(4,128)(2,1)S(1)} fusion(bf16[2,6,5,4,4,4,128]{6,5,4,3,2,1,0:T(4,128)(2,1)S(1)} %bitcast.129, bf16[2,6,5,4,4,4,128]{6,5,3,4,2,1,0:T(4,128)(2,1)S(1)} %copy.58, bf16[2,6,5,4,4,4,128]{6,5,4,3,2,1,0:T(4,128)(2,1)S(1)} %bitcast.130, pred[2,6]{1,0:T(4,128)(4,1)S(1)} %get-tuple-element.25, ...), kind=kLoop, calls=%fused_computation.38 | loop fusion | flops 1474560 | bytes 3932196 | tf_op jit(solution)/shard_map/jit(_where)/select_n | solution.py:39
  34.7 1.1 pad_maximum_fusion.1
  35.8 13.8 %collective-permute-done.2 = bf16[320,2240]{1,0:T(8,128)(2,1)S(1)} collective-permute-done((bf16[320,2240]{1,0:T(8,128)(2,1)}, bf16[320,2240]{1,0:T(8,128)(2,1)S(1)}, u32[]{:S(2)}, u32[]{:S(2)}) %collective-permute-start.2) | collective-permute-done | bytes 1433632 | tf_op jit(solution)/shard_map/ppermute | solution.py:29
  49.7 6.2 %collective-permute-done.3 = bf16[320,2240]{1,0:T(8,128)(2,1)} collective-permute-done((bf16[320,2240]{1,0:T(8,128)(2,1)}, bf16[320,2240]{1,0:T(8,128)(2,1)}, u32[]{:S(2)}, u32[]{:S(2)}) %collective-permute-start.3) | collective-permute-done | bytes 1433632 | tf_op jit(solution)/shard_map/ppermute | solution.py:29
  55.9 5.0 %pad_maximum_fusion = bf16[5,320,2240]{2,1,0:T(8,128)(2,1)} fusion(bf16[1,320,2240]{2,1,0:T(8,128)(2,1)} %bitcast.14, bf16[1,320,2240]{2,1,0:T(8,128)(2,1)S(1)} %bitcast.149, bf16[3,320,2240]{2,1,0:T(8,128)(2,1)S(1)} %bitcast.124), kind=kLoop, calls=%fused_computation.6 | loop fusion | flops 7168000 | bytes 14336000 | tf_op jit(solution)/shard_map/concatenate | solution.py:70
  60.9 3.8 %gather_fusion.1 = bf16[2,320,2240]{2,1,0:T(8,128)(2,1)S(1)} fusion(bf16[5,320,2240]{2,1,0:T(8,128)(2,1)} %pad_maximum_fusion, s32[1024]{0:T(1024)S(1)} %pad_clamp_fusion.1), kind=kCustom, calls=%fused_computation.5 | custom fusion | bytes 5734408 | tf_op jit(solution)/shard_map/jit(_take)/gather | solution.py:72
  64.7 3.1 %fusion.1 = f32[2,320,128]{2,1,0:T(8,128)S(1)} fusion(bf16[2,2240,128]{2,1,0:T(8,128)(2,1)} %bitcast.150, bf16[2,320,128]{2,1,0:T(8,128)(2,1)S(1)} %gather_fusion, pred[2]{0:T(512)(128)(4,1)S(1)} %compare_and_fusion.1, bf16[2,320,2240]{2,1,0:T(8,128)(2,1)S(1)} %gather_fusion.1), kind=kOutput, calls=%fused_computation.15 | convolution fusion | flops 368844800 | bytes 4505602 | tf_op jit(solution)/shard_map/nde,ner->ndr/dot_general | solution.py:51
  67.9 1.9 %collective-permute-start.7 = (bf16[1,2,320,128]{3,2,1,0:T(8,128)(2,1)S(1)}, bf16[1,2,320,128]{3,2,1,0:T(8,128)(2,1)S(1)}, u32[]{:S(2)}, u32[]{:S(2)}) collective-permute-start(bf16[1,2,320,128]{3,2,1,0:T(8,128)(2,1)S(1)} %get-tuple-element.21), channel_id=1, source_target_pairs={{16,0},{32,16},{48,32},{64,48},{80,64},{96,80},{112,96},{128,112},... | collective-permute-start | bytes 491528 | tf_op jit(solution)/shard_map/ppermute | solution.py:21
  69.9 2.4 %collective-permute-start.6 = (bf16[1,2,320,128]{3,2,1,0:T(8,128)(2,1)S(1)}, bf16[1,2,320,128]{3,2,1,0:T(8,128)(2,1)S(1)}, u32[]{:S(2)}, u32[]{:S(2)}) collective-permute-start(bf16[1,2,320,128]{3,2,1,0:T(8,128)(2,1)S(1)} %get-tuple-element.21), channel_id=1, source_target_pairs={{0,16},{16,32},{32,48},{48,64},{64,80},{80,96},{96,112},{112,128},... | collective-permute-start | bytes 491528 | tf_op jit(solution)/shard_map/ppermute | solution.py:18
  72.3 0.4 collective-permute-done.7
  72.7 5.0 %collective-permute-done.6 = bf16[1,2,320,128]{3,2,1,0:T(8,128)(2,1)S(1)} collective-permute-done((bf16[1,2,320,128]{3,2,1,0:T(8,128)(2,1)S(1)}, bf16[1,2,320,128]{3,2,1,0:T(8,128)(2,1)S(1)}, u32[]{:S(2)}, u32[]{:S(2)}) %collective-permute-start.6) | collective-permute-done | bytes 163872 | tf_op jit(solution)/shard_map/ppermute | solution.py:18
  77.7 0.1 pad_maximum_fusion.6
  77.8 0.7 gather_fusion.3
  78.5 0.2 broadcast_select_fusion.3
  78.7 0.4 copy.57
  79.2 1.4 %fusion.14 = bf16[2,6,5,4,4,4,128]{6,5,4,3,2,1,0:T(4,128)(2,1)S(1)} fusion(bf16[2,6,5,4,4,4,128]{6,5,4,3,2,1,0:T(4,128)(2,1)S(1)} %bitcast.132, bf16[2,6,5,4,4,4,128]{6,5,3,4,2,1,0:T(4,128)(2,1)S(1)} %copy.57, bf16[2,6,5,4,4,4,128]{6,5,4,3,2,1,0:T(4,128)(2,1)S(1)} %bitcast.135, pred[2,6]{1,0:T(4,128)(4,1)S(1)} %get-tuple-element.25, ...), kind=kLoop, calls=%fused_computation.35 | loop fusion | flops 1474560 | bytes 3932196 | tf_op jit(solution)/shard_map/jit(_where)/select_n | solution.py:39
  80.6 0.1 pad_maximum_fusion.2
  80.7 0.3 copy-done.1
  81.0 0.7 copy-done.6
  81.6 1.0 fusion.3
  82.7 1.9 %collective-permute-start.9 = (bf16[1,2,320,128]{3,2,1,0:T(8,128)(2,1)S(1)}, bf16[1,2,320,128]{3,2,1,0:T(8,128)(2,1)S(1)}, u32[]{:S(2)}, u32[]{:S(2)}) collective-permute-start(bf16[1,2,320,128]{3,2,1,0:T(8,128)(2,1)S(1)} %get-tuple-element.19), channel_id=1, source_target_pairs={{16,0},{32,16},{48,32},{64,48},{80,64},{96,80},{112,96},{128,112},... | collective-permute-start | bytes 491528 | tf_op jit(solution)/shard_map/ppermute | solution.py:21
  84.6 2.4 %collective-permute-start.8 = (bf16[1,2,320,128]{3,2,1,0:T(8,128)(2,1)S(1)}, bf16[1,2,320,128]{3,2,1,0:T(8,128)(2,1)S(1)}, u32[]{:S(2)}, u32[]{:S(2)}) collective-permute-start(bf16[1,2,320,128]{3,2,1,0:T(8,128)(2,1)S(1)} %get-tuple-element.19), channel_id=1, source_target_pairs={{0,16},{16,32},{32,48},{48,64},{64,80},{80,96},{96,112},{112,128},... | collective-permute-start | bytes 491528 | tf_op jit(solution)/shard_map/ppermute | solution.py:18
  87.0 0.4 collective-permute-done.9
  87.4 5.0 %collective-permute-done.8 = bf16[1,2,320,128]{3,2,1,0:T(8,128)(2,1)S(1)} collective-permute-done((bf16[1,2,320,128]{3,2,1,0:T(8,128)(2,1)S(1)}, bf16[1,2,320,128]{3,2,1,0:T(8,128)(2,1)S(1)}, u32[]{:S(2)}, u32[]{:S(2)}) %collective-permute-start.8) | collective-permute-done | bytes 163872 | tf_op jit(solution)/shard_map/ppermute | solution.py:18
  92.5 0.1 pad_maximum_fusion.7
  92.5 0.7 gather_fusion.4
  93.3 0.2 broadcast_select_fusion.2
  93.4 0.4 copy.56
  93.9 1.4 %fusion.12 = bf16[2,6,5,4,4,4,128]{6,5,4,3,2,1,0:T(4,128)(2,1)S(1)} fusion(bf16[2,6,5,4,4,4,128]{6,5,4,3,2,1,0:T(4,128)(2,1)S(1)} %bitcast.134, bf16[2,6,5,4,4,4,128]{6,5,3,4,2,1,0:T(4,128)(2,1)S(1)} %copy.56, bf16[2,6,5,4,4,4,128]{6,5,4,3,2,1,0:T(4,128)(2,1)S(1)} %bitcast.136, pred[2,6]{1,0:T(4,128)(4,1)S(1)} %get-tuple-element.25, ...), kind=kLoop, calls=%fused_computation.32 | loop fusion | flops 1474560 | bytes 3932196 | tf_op jit(solution)/shard_map/jit(_where)/select_n | solution.py:39
  95.3 0.1 pad_maximum_fusion.3
  95.4 0.3 copy-done.2
  95.7 1.0 fusion.5
  96.8 1.9 %collective-permute-start.11 = (bf16[1,2,320,128]{3,2,1,0:T(8,128)(2,1)S(1)}, bf16[1,2,320,128]{3,2,1,0:T(8,128)(2,1)S(1)}, u32[]{:S(2)}, u32[]{:S(2)}) collective-permute-start(bf16[1,2,320,128]{3,2,1,0:T(8,128)(2,1)S(1)} %get-tuple-element.17), channel_id=1, source_target_pairs={{16,0},{32,16},{48,32},{64,48},{80,64},{96,80},{112,96},{128,112},... | collective-permute-start | bytes 491528 | tf_op jit(solution)/shard_map/ppermute | solution.py:21
  98.7 2.6 %collective-permute-start.10 = (bf16[1,2,320,128]{3,2,1,0:T(8,128)(2,1)S(1)}, bf16[1,2,320,128]{3,2,1,0:T(8,128)(2,1)S(1)}, u32[]{:S(2)}, u32[]{:S(2)}) collective-permute-start(bf16[1,2,320,128]{3,2,1,0:T(8,128)(2,1)S(1)} %get-tuple-element.17), channel_id=1, source_target_pairs={{0,16},{16,32},{32,48},{48,64},{64,80},{80,96},{96,112},{112,128},... | collective-permute-start | bytes 491528 | tf_op jit(solution)/shard_map/ppermute | solution.py:18
  101.3 0.2 collective-permute-done.11
  101.5 5.0 %collective-permute-done.10 = bf16[1,2,320,128]{3,2,1,0:T(8,128)(2,1)S(1)} collective-permute-done((bf16[1,2,320,128]{3,2,1,0:T(8,128)(2,1)S(1)}, bf16[1,2,320,128]{3,2,1,0:T(8,128)(2,1)S(1)}, u32[]{:S(2)}, u32[]{:S(2)}) %collective-permute-start.10) | collective-permute-done | bytes 163872 | tf_op jit(solution)/shard_map/ppermute | solution.py:18
  106.5 0.1 pad_maximum_fusion.8
  106.6 0.7 gather_fusion.5
  107.3 0.2 broadcast_select_fusion.1
  107.5 0.4 copy.55
  108.0 1.4 %fusion.10 = bf16[2,6,5,4,4,4,128]{6,5,4,3,2,1,0:T(4,128)(2,1)S(1)} fusion(bf16[2,6,5,4,4,4,128]{6,5,4,3,2,1,0:T(4,128)(2,1)S(1)} %bitcast.126, bf16[2,6,5,4,4,4,128]{6,5,3,4,2,1,0:T(4,128)(2,1)S(1)} %copy.55, bf16[2,6,5,4,4,4,128]{6,5,4,3,2,1,0:T(4,128)(2,1)S(1)} %bitcast.127, pred[2,6]{1,0:T(4,128)(4,1)S(1)} %get-tuple-element.25, ...), kind=kLoop, calls=%fused_computation.29 | loop fusion | flops 1474560 | bytes 3932196 | tf_op jit(solution)/shard_map/jit(_where)/select_n | solution.py:39
  109.4 0.1 pad_maximum_fusion.4
  109.5 0.3 copy-done.3
  109.8 1.7 %fusion.8 = f32[1,1,2,320,128]{4,3,2,1,0:T(8,128)} fusion(f32[2,320,128]{2,1,0:T(8,128)S(1)} %fusion.5, bf16[2,2240,128]{2,1,0:T(8,128)(2,1)S(1)} %bitcast.151, bf16[2,320,128]{2,1,0:T(8,128)(2,1)S(1)} %gather_fusion, pred[2]{0:T(512)(128)(4,1)S(1)} %compare_and_fusion.1, bf16[2,320,2240]{2,1,0:T(8,128)(2,1)S(1)} %copy-done.3), kind=kOutput, calls=%fused_computation.22 | convolution fusion | flops 368844800 | bytes 4833282 | tf_op jit(solution)/shard_map/nde,ner->ndr/dot_general | solution.py:51
  (33 shorter events, 0.2 us)
Async XLA Ops:
  3.5 16.9 %collective-permute-start = (bf16[320,128]{1,0:T(8,128)(2,1)S(1)}, bf16[320,128]{1,0:T(8,128)(2,1)S(1)}, u32[]{:S(2)}, u32[]{:S(2)}) collective-permute-start(bf16[320,128]{1,0:T(8,128)(2,1)S(1)} %get-tuple-element.22), channel_id=1, source_target_pairs={{0,1},{1,2},{2,3},{3,4},{4,5},{5,6},{6,7},{7,8},{8,9},{9,10},{10,1... | collective-permute-start | bytes 245768 | tf_op jit(solution)/shard_map/ppermute | solution.py:29
  6.6 13.7 %copy-start.9 = (s32[1,1,2]{2,1,0:T(1,128)S(1)}, s32[1,1,2]{2,1,0:T(1,128)}, u32[]{:S(2)}) copy-start(s32[1,1,2]{2,1,0:T(1,128)} %param.11) | copy-start | bytes 28
  6.6 13.7 %copy-start.7 = (s32[1,1,2,6]{3,2,1,0:T(2,128)S(1)}, s32[1,1,2,6]{3,2,1,0:T(2,128)}, u32[]{:S(2)}) copy-start(s32[1,1,2,6]{3,2,1,0:T(2,128)} %param.12) | copy-start | bytes 148
  6.6 13.8 %copy-start.8 = (s32[1,1,2,6]{3,2,1,0:T(2,128)S(1)}, s32[1,1,2,6]{3,2,1,0:T(2,128)}, u32[]{:S(2)}) copy-start(s32[1,1,2,6]{3,2,1,0:T(2,128)} %param.13) | copy-start | bytes 148
  6.6 13.9 %copy-start.4 = (bf16[1,1,3,320,128]{4,3,2,1,0:T(8,128)(2,1)S(1)}, bf16[1,1,3,320,128]{4,3,2,1,0:T(8,128)(2,1)}, u32[]{:S(2)}) copy-start(bf16[1,1,3,320,128]{4,3,2,1,0:T(8,128)(2,1)} %param.9) | copy-start | bytes 737284
  6.6 13.8 %collective-permute-start.1 = (bf16[320,128]{1,0:T(8,128)(2,1)S(1)}, bf16[320,128]{1,0:T(8,128)(2,1)S(1)}, u32[]{:S(2)}, u32[]{:S(2)}) collective-permute-start(bf16[320,128]{1,0:T(8,128)(2,1)S(1)} %get-tuple-element.23), channel_id=1, source_target_pairs={{1,0},{2,1},{3,2},{4,3},{5,4},{6,5},{7,6},{8,7},{9,8},{10,9},{11,1... | collective-permute-start | bytes 245768 | tf_op jit(solution)/shard_map/ppermute | solution.py:29
  13.2 36.4 %collective-permute-start.2 = (bf16[320,2240]{1,0:T(8,128)(2,1)}, bf16[320,2240]{1,0:T(8,128)(2,1)S(1)}, u32[]{:S(2)}, u32[]{:S(2)}) collective-permute-start(bf16[320,2240]{1,0:T(8,128)(2,1)} %get-tuple-element.6), channel_id=1, source_target_pairs={{0,1},{1,2},{2,3},{3,4},{4,5},{5,6},{6,7},{7,8},{8,9},{9,10},{10,1... | collective-permute-start | bytes 4300808 | tf_op jit(solution)/shard_map/ppermute | solution.py:29
  18.3 37.6 %collective-permute-start.3 = (bf16[320,2240]{1,0:T(8,128)(2,1)}, bf16[320,2240]{1,0:T(8,128)(2,1)}, u32[]{:S(2)}, u32[]{:S(2)}) collective-permute-start(bf16[320,2240]{1,0:T(8,128)(2,1)} %get-tuple-element.7), channel_id=1, source_target_pairs={{1,0},{2,1},{3,2},{4,3},{5,4},{6,5},{7,6},{8,7},{9,8},{10,9},{11,1... | collective-permute-start | bytes 4300808 | tf_op jit(solution)/shard_map/ppermute | solution.py:29
  21.2 5.6 %collective-permute-start.5 = (bf16[1,2,320,128]{3,2,1,0:T(8,128)(2,1)S(1)}, bf16[1,2,320,128]{3,2,1,0:T(8,128)(2,1)S(1)}, u32[]{:S(2)}, u32[]{:S(2)}) collective-permute-start(bf16[1,2,320,128]{3,2,1,0:T(8,128)(2,1)S(1)} %multiply_convert_fusion), channel_id=1, source_target_pairs={{16,0},{32,16},{48,32},{64,48},{80,64},{96,80},{112,96},{128,112},... | collective-permute-start | bytes 491528 | tf_op jit(solution)/shard_map/ppermute | solution.py:21
  24.0 7.8 %collective-permute-start.4 = (bf16[1,2,320,128]{3,2,1,0:T(8,128)(2,1)S(1)}, bf16[1,2,320,128]{3,2,1,0:T(8,128)(2,1)S(1)}, u32[]{:S(2)}, u32[]{:S(2)}) collective-permute-start(bf16[1,2,320,128]{3,2,1,0:T(8,128)(2,1)S(1)} %multiply_convert_fusion), channel_id=1, source_target_pairs={{0,16},{16,32},{32,48},{48,64},{64,80},{80,96},{96,112},{112,128},... | collective-permute-start | bytes 491528 | tf_op jit(solution)/shard_map/ppermute | solution.py:18
  31.9 24.0 %slice-start = ((s8[4423680]{0:T(1024)(128)(4,1)}), s8[229376]{0:T(1024)(128)(4,1)S(1)}, s32[]{:S(2)}) async-start(s8[4423680]{0:T(1024)(128)(4,1)} %bitcast.122), calls=%async_computation | async-start | bytes 458752
  32.8 23.0 %slice-start.1 = ((s8[4423680]{0:T(1024)(128)(4,1)}), s8[4194304]{0:T(1024)(128)(4,1)S(1)}, s32[]{:S(2)}) async-start(s8[4423680]{0:T(1024)(128)(4,1)} %bitcast.122), calls=%async_computation.1 | async-start | bytes 8388608
  64.7 3.1 %copy-start = (bf16[2,320,2240]{2,1,0:T(8,128)(2,1)}, bf16[2,320,2240]{2,1,0:T(8,128)(2,1)S(1)}, u32[]{:S(2)}) copy-start(bf16[2,320,2240]{2,1,0:T(8,128)(2,1)S(1)} %gather_fusion.1) | copy-start | bytes 8601604
  67.8 9.9 %copy-start.5 = (f32[2,320,128]{2,1,0:T(8,128)}, f32[2,320,128]{2,1,0:T(8,128)S(1)}, u32[]{:S(2)}) copy-start(f32[2,320,128]{2,1,0:T(8,128)S(1)} %fusion.1) | copy-start | bytes 983044
  67.9 4.8 %collective-permute-start.7 = (bf16[1,2,320,128]{3,2,1,0:T(8,128)(2,1)S(1)}, bf16[1,2,320,128]{3,2,1,0:T(8,128)(2,1)S(1)}, u32[]{:S(2)}, u32[]{:S(2)}) collective-permute-start(bf16[1,2,320,128]{3,2,1,0:T(8,128)(2,1)S(1)} %get-tuple-element.21), channel_id=1, source_target_pairs={{16,0},{32,16},{48,32},{64,48},{80,64},{96,80},{112,96},{128,112},... | collective-permute-start | bytes 491528 | tf_op jit(solution)/shard_map/ppermute | solution.py:21
  69.9 7.8 %collective-permute-start.6 = (bf16[1,2,320,128]{3,2,1,0:T(8,128)(2,1)S(1)}, bf16[1,2,320,128]{3,2,1,0:T(8,128)(2,1)S(1)}, u32[]{:S(2)}, u32[]{:S(2)}) collective-permute-start(bf16[1,2,320,128]{3,2,1,0:T(8,128)(2,1)S(1)} %get-tuple-element.21), channel_id=1, source_target_pairs={{0,16},{16,32},{32,48},{48,64},{64,80},{80,96},{96,112},{112,128},... | collective-permute-start | bytes 491528 | tf_op jit(solution)/shard_map/ppermute | solution.py:18
  79.1 1.8 %copy-start.1 = (bf16[2,320,2240]{2,1,0:T(8,128)(2,1)S(1)}, bf16[2,320,2240]{2,1,0:T(8,128)(2,1)}, u32[]{:S(2)}) copy-start(bf16[2,320,2240]{2,1,0:T(8,128)(2,1)} %copy-done) | copy-start | bytes 8601604
  80.6 1.1 copy-start.6
  82.7 4.7 %collective-permute-start.9 = (bf16[1,2,320,128]{3,2,1,0:T(8,128)(2,1)S(1)}, bf16[1,2,320,128]{3,2,1,0:T(8,128)(2,1)S(1)}, u32[]{:S(2)}, u32[]{:S(2)}) collective-permute-start(bf16[1,2,320,128]{3,2,1,0:T(8,128)(2,1)S(1)} %get-tuple-element.19), channel_id=1, source_target_pairs={{16,0},{32,16},{48,32},{64,48},{80,64},{96,80},{112,96},{128,112},... | collective-permute-start | bytes 491528 | tf_op jit(solution)/shard_map/ppermute | solution.py:21
  84.6 7.8 %collective-permute-start.8 = (bf16[1,2,320,128]{3,2,1,0:T(8,128)(2,1)S(1)}, bf16[1,2,320,128]{3,2,1,0:T(8,128)(2,1)S(1)}, u32[]{:S(2)}, u32[]{:S(2)}) collective-permute-start(bf16[1,2,320,128]{3,2,1,0:T(8,128)(2,1)S(1)} %get-tuple-element.19), channel_id=1, source_target_pairs={{0,16},{16,32},{32,48},{48,64},{64,80},{80,96},{96,112},{112,128},... | collective-permute-start | bytes 491528 | tf_op jit(solution)/shard_map/ppermute | solution.py:18
  93.9 1.8 %copy-start.2 = (bf16[2,320,2240]{2,1,0:T(8,128)(2,1)S(1)}, bf16[2,320,2240]{2,1,0:T(8,128)(2,1)}, u32[]{:S(2)}) copy-start(bf16[2,320,2240]{2,1,0:T(8,128)(2,1)} %copy-done) | copy-start | bytes 8601604
  96.8 4.7 %collective-permute-start.11 = (bf16[1,2,320,128]{3,2,1,0:T(8,128)(2,1)S(1)}, bf16[1,2,320,128]{3,2,1,0:T(8,128)(2,1)S(1)}, u32[]{:S(2)}, u32[]{:S(2)}) collective-permute-start(bf16[1,2,320,128]{3,2,1,0:T(8,128)(2,1)S(1)} %get-tuple-element.17), channel_id=1, source_target_pairs={{16,0},{32,16},{48,32},{64,48},{80,64},{96,80},{112,96},{128,112},... | collective-permute-start | bytes 491528 | tf_op jit(solution)/shard_map/ppermute | solution.py:21
  98.7 7.8 %collective-permute-start.10 = (bf16[1,2,320,128]{3,2,1,0:T(8,128)(2,1)S(1)}, bf16[1,2,320,128]{3,2,1,0:T(8,128)(2,1)S(1)}, u32[]{:S(2)}, u32[]{:S(2)}) collective-permute-start(bf16[1,2,320,128]{3,2,1,0:T(8,128)(2,1)S(1)} %get-tuple-element.17), channel_id=1, source_target_pairs={{0,16},{16,32},{32,48},{48,64},{64,80},{80,96},{96,112},{112,128},... | collective-permute-start | bytes 491528 | tf_op jit(solution)/shard_map/ppermute | solution.py:18
  107.9 1.8 %copy-start.3 = (bf16[2,320,2240]{2,1,0:T(8,128)(2,1)S(1)}, bf16[2,320,2240]{2,1,0:T(8,128)(2,1)}, u32[]{:S(2)}) copy-start(bf16[2,320,2240]{2,1,0:T(8,128)(2,1)} %copy-done) | copy-start | bytes 8601604
where the time goes:
time: 112 us; the launch traced here: 111 us
  waiting for transfers between devices  42 us (38%)
  starting transfers between devices  30.9 us (28%)
  local copies, waits for them, and re-layouts  16.8 us (15%)
  other arithmetic  13.3 us (12%)
  matrix products  6.75 us (6%)
  between operations  1.75 us (2%)
    ppermute x4, waiting for transfers between devices, with_halo(): lax.ppermute(lax.slice_in_dim(block, block.shape[dim] - width, None, axis...  20.1 us
    ppermute x4, waiting for transfers between devices, from_behind(): lax.ppermute(value, axis, [(source, source + steps) for source in range(l...  20.1 us
    ppermute x4, starting transfers between devices, from_behind(): lax.ppermute(value, axis, [(source, source + steps) for source in range(l...  13 us
    ppermute x4, starting transfers between devices, with_halo(): lax.ppermute(lax.slice_in_dim(block, block.shape[dim] - width, None, axis...  9.29 us
    ppermute x4, starting transfers between devices, with_halo(): lax.ppermute(lax.slice_in_dim(block, 0, width, axis=dim), axis, backward)  8.59 us
    dot_general x4, matrix products, coupled(): jnp.einsum('nde,ner->ndr', row_blocks, stacked, preferred_element_type=jn...  6.75 us
    select_n x4, other arithmetic, turned_faces(): jnp.where((face_codes == quarter)[:, :, None, None, None, None, None], jn...  5.62 us
    concatenate x1, other arithmetic, shards(): jnp.concatenate([local_blocks, from_lower[0][None], from_upper[0][None]],...  5.01 us
  transfers between devices with their start and end apart: 12, of which 10 were waited for; matrix products, arithmetic and copies ran while one was open for 8% of the time, Pallas kernels for 0%

commit v1 on v0

v1 whole, which is shorter than its diff:
```python
import jax
import jax.numpy as jnp
from jax import lax
from jax.experimental import pallas as pl
from jax.experimental.pallas import tpu as pltpu
from jax.sharding import PartitionSpec as P

DOF = 320
FACES = 6
RHS = 128
KEPT = 2
ITERS = 4
RELAXATION = 0.7
WIDE = 7 * DOF
TILE = 128
SLOTS = 6
MERGED = SLOTS * DOF
TILES = MERGED // TILE
HEAD = 2
META = 16


def vmem(shape, dtype):
    return pltpu.VMEM(shape, dtype)


def near(*arrays):
    return tuple(pltpu.with_memory_space_constraint(array, pltpu.VMEM) for array in arrays)


def far(*arrays):
    return tuple(pltpu.with_memory_space_constraint(array, pltpu.HBM) for array in arrays)


PARAMS = pltpu.CompilerParams(vmem_limit_bytes=20 * 2**20)

SMEM_SPEC = pl.BlockSpec(memory_space=pltpu.SMEM)
VMEM_SPEC = pl.BlockSpec(memory_space=pltpu.VMEM)
ANY_SPEC = pl.BlockSpec(memory_space=pl.ANY)


def merge_row(row_ref, neighbor, turn, row, parity, acc_ref):
    lane = lax.broadcasted_iota(jnp.int32, (DOF, TILE), 1)
    for tile in range(HEAD):
        acc_ref[tile] = row_ref[:, tile * TILE : (tile + 1) * TILE].astype(jnp.float32)
    edge = row_ref[:, HEAD * TILE : (HEAD + 1) * TILE].astype(jnp.float32)
    acc_ref[HEAD] = jnp.where(lane < DOF - HEAD * TILE, edge, 0.0)
    for tile in range(HEAD + 1, TILES):
        acc_ref[tile] = jnp.zeros((DOF, TILE), jnp.float32)
    for face in range(FACES):
        start = DOF * (face + 1)
        shift = start % TILE
        base = start - shift
        width = DOF + shift
        n = neighbor(face)
        k = turn(face)
        layer = n // 2
        which = n % 2
        first = jnp.where(parity == 0, layer == 2, layer == 0)
        slot = jnp.where(layer == 1, 1, jnp.where(first, 2, 4) + which)
        place = DOF * slot
        tile = place // TILE
        offset = place - tile * TILE
        column = lax.broadcasted_iota(jnp.int32, (1, 3 * TILE), 1) - offset
        a = (column // 16) % 4
        b = (column // 4) % 4
        source_a = jnp.where(k == 0, a, jnp.where(k == 1, 3 - b, jnp.where(k == 2, 3 - a, b)))
        source_b = jnp.where(k == 0, b, jnp.where(k == 1, a, jnp.where(k == 2, 3 - b, 3 - a)))
        source = shift + (column // 64) * 64 + source_a * 16 + source_b * 4 + column % 4
        source = jnp.where((column >= 0) & (column < DOF), source, -1)
        rows = lax.broadcasted_iota(jnp.int32, (width, 3 * TILE), 0)
        select = jnp.where(rows == source, 1.0, 0.0).astype(jnp.bfloat16)
        moved = jnp.dot(row_ref[:, base : base + width], select, preferred_element_type=jnp.float32)
        for part in range(3):
            acc_ref[tile + part] += moved[:, part * TILE : (part + 1) * TILE]


def pick_kernel(departure, arrival, neighbors, orientation, blocks, rhs, head, row, meta_down, meta_up, sems):
    slot = jnp.maximum(jnp.maximum(departure[0, 0, 0], departure[0, 0, 1]), 0)
    whole = pltpu.make_async_copy(blocks.at[0, 0, slot], row, sems.at[0])
    side = pltpu.make_async_copy(rhs.at[0, 0, slot], head.at[:, 0:RHS], sems.at[1])
    whole.start()
    side.start()
    for meta, code in ((meta_down, 3), (meta_up, 4)):
        q = jnp.where(arrival[0, 0, 1] == code, 1, 0)
        for face in range(FACES):
            meta[face] = neighbors[0, 0, q, face]
            meta[FACES + face] = orientation[0, 0, q, face]
        for index in range(2 * FACES, META):
            meta[index] = q
    whole.wait()
    side.wait()
    head[:, RHS:] = row[:, 0 : HEAD * TILE]


def pick(departure, arrival, neighbors, orientation, blocks, rhs):
    return pl.pallas_call(
        pick_kernel,
        in_specs=[SMEM_SPEC] * 4 + [ANY_SPEC] * 2,
        out_specs=[VMEM_SPEC, VMEM_SPEC, SMEM_SPEC, SMEM_SPEC],
        out_shape=[
            vmem((DOF, RHS + HEAD * TILE), jnp.bfloat16),
            vmem((DOF, WIDE), jnp.bfloat16),
            jax.ShapeDtypeStruct((META,), jnp.int32),
            jax.ShapeDtypeStruct((META,), jnp.int32),
        ],
        scratch_shapes=[pltpu.SemaphoreType.DMA((2,))],
        compiler_params=PARAMS,
        name="pick",
    )(*far(departure, arrival, neighbors, orientation, blocks, rhs))


def send_kernel(departure, from_upper, from_lower, row, tail, acc):
    parity = lax.axis_index("gx") % 2
    up = departure[0, 0, 1] >= 0

    def entry(index):
        return jnp.where(up, from_upper[index], from_lower[index])

    merge_row(row, entry, lambda face: entry(FACES + face), entry(2 * FACES), parity, acc)
    for tile in range(HEAD, TILES):
        tail[:, (tile - HEAD) * TILE : (tile - HEAD + 1) * TILE] = acc[tile].astype(jnp.bfloat16)


def merged_tail(departure, from_upper, from_lower, row):
    return pl.pallas_call(
        send_kernel,
        in_specs=[SMEM_SPEC] * 3 + [VMEM_SPEC],
        out_specs=VMEM_SPEC,
        out_shape=vmem((DOF, (TILES - HEAD) * TILE), jnp.bfloat16),
        scratch_shapes=[pltpu.VMEM((TILES, DOF, TILE), jnp.float32)],
        compiler_params=PARAMS,
        name="merge_tail",
    )(departure, from_upper, from_lower, *near(row))


def first_kernel(arrival, rhs, lower, upper, kept, rounded):
    for q in range(KEPT):
        source = arrival[0, 0, q]

        @pl.when(source < 3)
        def _():
            kept[q] = rhs[0, 0, jnp.clip(source, 0, 2)]

        @pl.when(source == 3)
        def _():
            kept[q] = lower[:, 0:RHS]

        @pl.when(source == 4)
        def _():
            kept[q] = upper[:, 0:RHS]

        rounded[q] = (RELAXATION * kept[q].astype(jnp.float32)).astype(jnp.bfloat16)


def first(arrival, rhs, lower, upper):
    pair = vmem((KEPT, DOF, RHS), jnp.bfloat16)
    return pl.pallas_call(
        first_kernel,
        in_specs=[SMEM_SPEC] + [VMEM_SPEC] * 3,
        out_specs=[VMEM_SPEC] * 2,
        out_shape=[pair, pair],
        compiler_params=PARAMS,
        name="first",
    )(arrival, *near(rhs, lower, upper))


def local_kernel(arrival, neighbors, orientation, blocks, merged, rows, acc, sems):
    parity = lax.axis_index("gx") % 2
    copies = [
        pltpu.make_async_copy(blocks.at[0, 0, jnp.clip(arrival[0, 0, q], 0, 2)], rows.at[q], sems.at[q])
        for q in range(KEPT)
    ]
    for copy in copies:
        copy.start()
    for q in range(KEPT):
        copies[q].wait()
        merge_row(
            rows.at[q], lambda face: neighbors[0, 0, q, face], lambda face: orientation[0, 0, q, face], q, parity, acc
        )
        for tile in range(TILES):
            merged[q, :, tile * TILE : (tile + 1) * TILE] = acc[tile].astype(jnp.bfloat16)


def merged_local(arrival, neighbors, orientation, blocks):
    return pl.pallas_call(
        local_kernel,
        in_specs=[SMEM_SPEC] * 3 + [ANY_SPEC],
        out_specs=VMEM_SPEC,
        out_shape=vmem((KEPT, DOF, MERGED), jnp.bfloat16),
        scratch_shapes=[
            pltpu.VMEM((KEPT, DOF, WIDE), jnp.bfloat16),
            pltpu.VMEM((TILES, DOF, TILE), jnp.float32),
            pltpu.SemaphoreType.DMA((KEPT,)),
        ],
        compiler_params=PARAMS,
        name="merge_local",
    )(arrival, neighbors, orientation, *far(blocks))


def applied_rows(merged, own, pair_a, pair_b):
    far = jnp.concatenate([pair_a[0], pair_a[1], pair_b[0], pair_b[1]], axis=0)
    for q in range(KEPT):
        near = jnp.concatenate([own[q], own[1 - q]], axis=0)
        applied = jnp.dot(merged[q, :, 0 : 2 * DOF], near, preferred_element_type=jnp.float32)
        applied += jnp.dot(merged[q, :, 2 * DOF :], far, preferred_element_type=jnp.float32)
        yield q, applied


def opening_kernel(arrival, local, lo_head, lo_tail, hi_head, hi_tail, kept, own, pair_a, pair_b, merged, iterate, rounded):
    for q in range(KEPT):
        source = arrival[0, 0, q]
        for code, head, tail in ((3, lo_head, lo_tail), (4, hi_head, hi_tail)):

            @pl.when(source == code)
            def _():
                merged[q, :, 0 : HEAD * TILE] = head[:, RHS:]
                merged[q, :, HEAD * TILE :] = tail[...]

        @pl.when(source < 3)
        def _():
            merged[q] = local[q]

    for q, applied in applied_rows(merged, own, pair_a, pair_b):
        side = kept[q].astype(jnp.float32)
        value = RELAXATION * side + RELAXATION * (side - applied)
        iterate[q] = value
        rounded[q] = value.astype(jnp.bfloat16)


def opening(arrival, local, lo_head, lo_tail, hi_head, hi_tail, kept, own, pair_a, pair_b):
    return pl.pallas_call(
        opening_kernel,
        in_specs=[SMEM_SPEC] + [VMEM_SPEC] * 9,
        out_specs=[VMEM_SPEC] * 3,
        out_shape=[
            vmem((KEPT, DOF, MERGED), jnp.bfloat16),
            vmem((KEPT, DOF, RHS), jnp.float32),
            vmem((KEPT, DOF, RHS), jnp.bfloat16),
        ],
        compiler_params=PARAMS,
        name="opening",
    )(arrival, *near(local, lo_head, lo_tail, hi_head, hi_tail, kept, own, pair_a, pair_b))


def middle_kernel(merged, kept, iterate, own, pair_a, pair_b, iterate_out, rounded):
    for q, applied in applied_rows(merged, own, pair_a, pair_b):
        value = iterate[q] + RELAXATION * (kept[q].astype(jnp.float32) - applied)
        iterate_out[q] = value
        rounded[q] = value.astype(jnp.bfloat16)


def middle(merged, kept, iterate, own, pair_a, pair_b):
    return pl.pallas_call(
        middle_kernel,
        in_specs=[VMEM_SPEC] * 6,
        out_specs=[VMEM_SPEC] * 2,
        out_shape=[vmem((KEPT, DOF, RHS), jnp.float32), vmem((KEPT, DOF, RHS), jnp.bfloat16)],
        compiler_params=PARAMS,
        name="middle",
    )(*near(merged, kept, iterate, own, pair_a, pair_b))


def closing_kernel(merged, kept, iterate, own, pair_a, pair_b, smoothed):
    for q, applied in applied_rows(merged, own, pair_a, pair_b):
        smoothed[0, 0, q] = iterate[q] + RELAXATION * (kept[q].astype(jnp.float32) - applied)


def closing(merged, kept, iterate, own, pair_a, pair_b):
    return pl.pallas_call(
        closing_kernel,
        in_specs=[VMEM_SPEC] * 6,
        out_specs=VMEM_SPEC,
        out_shape=jax.ShapeDtypeStruct((1, 1, KEPT, DOF, RHS), jnp.float32),
        compiler_params=PARAMS,
        name="closing",
    )(*near(merged, kept, iterate, own, pair_a, pair_b))


def shifted(value, axis, steps):
    count = lax.axis_size(axis)
    leading, last = (max(0, -steps), min(count, count - steps))
    return lax.ppermute(value, axis, [(source, source + steps) for source in range(leading, last)])


def swapped(value, axis, start):
    count = lax.axis_size(axis)
    pairs = []
    for low in range(start, count - 1, 2):
        pairs += [(low, low + 1), (low + 1, low)]
    return lax.ppermute(value, axis, pairs)


def halo(rounded):
    pair_b = swapped(rounded, "gx", 1)
    pair_a = swapped(rounded, "gx", 0)
    return pair_a, pair_b


def shards(blocks, right_side, departure, arrival, neighbors, orientation):
    head, row, meta_down, meta_up = pick(departure, arrival, neighbors, orientation, blocks, right_side)
    meta_upper = shifted(meta_down, "gy", -1)
    meta_lower = shifted(meta_up, "gy", 1)
    lo_head = shifted(head, "gy", 1)
    hi_head = shifted(head, "gy", -1)
    tail = merged_tail(departure, meta_upper, meta_lower, row)
    lo_tail = shifted(tail, "gy", 1)
    hi_tail = shifted(tail, "gy", -1)
    kept, own = first(arrival, right_side, lo_head, hi_head)
    pair_a, pair_b = halo(own)
    local = merged_local(arrival, neighbors, orientation, blocks)
    merged, iterate, own = opening(
        arrival, local, lo_head, lo_tail, hi_head, hi_tail, kept, own, pair_a, pair_b
    )
    for _ in range(ITERS - 2):
        pair_a, pair_b = halo(own)
        iterate, own = middle(merged, kept, iterate, own, pair_a, pair_b)
    pair_a, pair_b = halo(own)
    return closing(merged, kept, iterate, own, pair_a, pair_b)


def solution(mesh):
    in_specs = (
        P("gx", "gy", None, None, None),
        P("gx", "gy", None, None, None),
        P("gx", "gy", None),
        P("gx", "gy", None),
        P("gx", "gy", None, None),
        P("gx", "gy", None, None),
    )
    out_specs = P("gx", "gy", None, None, None)
    return jax.shard_map(shards, mesh=mesh, in_specs=in_specs, out_specs=out_specs, check_vma=False)
```

time: 112 us -> 94.4 us (0.84)
  the two profiles are of different devices: /device:TPU:410 before, /device:TPU:231 now
where the time goes in v1:
time: 94.4 us; the launch traced here: 93.8 us
  starting transfers between devices  42.6 us (45%)
  waiting for transfers between devices  36.1 us (38%)
  Pallas kernels  14.9 us (16%)
    ppermute x6, waiting for transfers between devices, shifted(): lax.ppermute(value, axis, [(source, source + steps) for source in range(l...  27.4 us
    ppermute x8, starting transfers between devices, swapped(): return lax.ppermute(value, axis, pairs)  24.4 us
    ppermute x6, starting transfers between devices, shifted(): lax.ppermute(value, axis, [(source, source + steps) for source in range(l...  18.2 us
    ppermute x8, waiting for transfers between devices, swapped(): return lax.ppermute(value, axis, pairs)  8.67 us
    pallas_call x1, Pallas kernels, merged_local(): pl.pallas_call(local_kernel, in_specs=[SMEM_SPEC] * 3 + [ANY_SPEC], out_s...  4.82 us
    pallas_call x1, Pallas kernels, pick(): pl.pallas_call(pick_kernel, in_specs=[SMEM_SPEC] * 4 + [ANY_SPEC] * 2, ou...  2.85 us
    pallas_call x1, Pallas kernels, merged_tail(): pl.pallas_call(send_kernel, in_specs=[SMEM_SPEC] * 3 + [VMEM_SPEC], out_s...  1.98 us
  transfers between devices with their start and end apart: 14, of which 6 were waited for; matrix products, arithmetic and copies ran while one was open for 0% of the time, Pallas kernels for 6%

profile of v1, /device:TPU:231, one launch (start us, length us, event | category | flops | bytes accessed | tf_op | source)
XLA Modules:
  0.0 93.8 jit_solution(13806117236423934689)
XLA Ops:
  0.0 0.0 copy-start.4
  0.0 2.9 %pick.1 = (bf16[320,384]{1,0:T(8,128)(2,1)S(1)}, bf16[320,2240]{1,0:T(8,128)(2,1)S(1)}, s32[16]{0:T(128)S(1)}, s32[16]{0:T(128)S(1)}) custom-call(s32[1,1,2]{2,1,0:T(1,128)} %departure.3, s32[1,1,2]{2,1,0:T(1,128)} %arrival.7, s32[1,1,2,6]{3,2,1,0:T(2,128)} %neighbors.3, s32[1,1,2,6]{3,2,1,0:T(2,128)} %orientation.3, bf16[1,1,3,320,2240]{4,3,2,1,0:T(8,128)(2,1)} %blocks.3, ...), custom_call_target="tpu_custom_call" | custom-call | tf_op jit(solution)/shard_map/pick/pallas_call | solution.py:97
  2.9 0.0 copy-start
  2.9 0.0 copy-start.1
  2.9 5.0 %collective-permute-start.1 = (s32[16]{0:T(128)S(1)}, s32[16]{0:T(128)S(1)}, u32[]{:S(2)}, u32[]{:S(2)}) collective-permute-start(s32[16]{0:T(128)S(1)} %get-tuple-element.19), channel_id=1, source_target_pairs={{1,0},{2,1},{3,2},{4,3},{5,4},{6,5},{7,6},{8,7},{9,8},{10,9},{11,1... | collective-permute-start | bytes 200 | tf_op jit(solution)/shard_map/ppermute | solution.py:283
  7.9 1.9 %collective-permute-start.2 = (s32[16]{0:T(128)S(1)}, s32[16]{0:T(128)S(1)}, u32[]{:S(2)}, u32[]{:S(2)}) collective-permute-start(s32[16]{0:T(128)S(1)} %get-tuple-element.20), channel_id=1, source_target_pairs={{0,1},{1,2},{2,3},{3,4},{4,5},{5,6},{6,7},{7,8},{8,9},{9,10},{10,1... | collective-permute-start | bytes 200 | tf_op jit(solution)/shard_map/ppermute | solution.py:283
  9.9 0.0 collective-permute-done.1.from_upper
  9.9 4.5 %collective-permute-done.2.from_lower = s32[16]{0:T(128)S(1)} collective-permute-done((s32[16]{0:T(128)S(1)}, s32[16]{0:T(128)S(1)}, u32[]{:S(2)}, u32[]{:S(2)}) %collective-permute-start.2) | collective-permute-done | bytes 96 | tf_op jit(solution)/shard_map/ppermute | solution.py:283
  14.4 0.0 copy-done.4
  14.4 0.0 copy-start.2
  14.4 0.0 copy-start.3
  14.4 2.0 %merge_tail.1 = bf16[320,1664]{1,0:T(8,128)(2,1)S(1)} custom-call(s32[1,1,2]{2,1,0:T(1,128)S(1)} %copy-done.4, s32[16]{0:T(128)S(1)} %collective-permute-done.1.from_upper, s32[16]{0:T(128)S(1)} %collective-permute-done.2.from_lower, bf16[320,2240]{1,0:T(8,128)(2,1)S(1)} %get-tuple-element.21.row), custom_call_target="tpu_custom_call" | custom-call | tf_op jit(solution)/shard_map/merge_tail/pallas_call | solution.py:126
  16.4 1.9 %collective-permute-start.5 = (bf16[320,1664]{1,0:T(8,128)(2,1)S(1)}, bf16[320,1664]{1,0:T(8,128)(2,1)S(1)}, u32[]{:S(2)}, u32[]{:S(2)}) collective-permute-start(bf16[320,1664]{1,0:T(8,128)(2,1)S(1)} %merge_tail.1), channel_id=1, source_target_pairs={{1,0},{2,1},{3,2},{4,3},{5,4},{6,5},{7,6},{8,7},{9,8},{10,9},{11,1... | collective-permute-start | bytes 3194888 | tf_op jit(solution)/shard_map/ppermute | solution.py:283
  18.3 3.4 %collective-permute-start.3 = (bf16[320,1664]{1,0:T(8,128)(2,1)S(1)}, bf16[320,1664]{1,0:T(8,128)(2,1)S(1)}, u32[]{:S(2)}, u32[]{:S(2)}) collective-permute-start(bf16[320,1664]{1,0:T(8,128)(2,1)S(1)} %merge_tail.1), channel_id=1, source_target_pairs={{0,1},{1,2},{2,3},{3,4},{4,5},{5,6},{6,7},{7,8},{8,9},{9,10},{10,1... | collective-permute-start | bytes 3194888 | tf_op jit(solution)/shard_map/ppermute | solution.py:283
  21.7 4.0 %collective-permute-start.4 = (bf16[320,384]{1,0:T(8,128)(2,1)S(1)}, bf16[320,384]{1,0:T(8,128)(2,1)S(1)}, u32[]{:S(2)}, u32[]{:S(2)}) collective-permute-start(bf16[320,384]{1,0:T(8,128)(2,1)S(1)} %get-tuple-element.18), channel_id=1, source_target_pairs={{1,0},{2,1},{3,2},{4,3},{5,4},{6,5},{7,6},{8,7},{9,8},{10,9},{11,1... | collective-permute-start | bytes 737288 | tf_op jit(solution)/shard_map/ppermute | solution.py:283
  25.7 1.9 %collective-permute-start = (bf16[320,384]{1,0:T(8,128)(2,1)S(1)}, bf16[320,384]{1,0:T(8,128)(2,1)S(1)}, u32[]{:S(2)}, u32[]{:S(2)}) collective-permute-start(bf16[320,384]{1,0:T(8,128)(2,1)S(1)} %get-tuple-element.18), channel_id=1, source_target_pairs={{0,1},{1,2},{2,3},{3,4},{4,5},{5,6},{6,7},{7,8},{8,9},{9,10},{10,1... | collective-permute-start | bytes 737288 | tf_op jit(solution)/shard_map/ppermute | solution.py:283
  27.6 18.9 %collective-permute-done.4.upper.hi_head = bf16[320,384]{1,0:T(8,128)(2,1)S(1)} collective-permute-done((bf16[320,384]{1,0:T(8,128)(2,1)S(1)}, bf16[320,384]{1,0:T(8,128)(2,1)S(1)}, u32[]{:S(2)}, u32[]{:S(2)}) %collective-permute-start.4) | collective-permute-done | bytes 245792 | tf_op jit(solution)/shard_map/ppermute | solution.py:283
  46.5 4.0 %collective-permute-done.lower.lo_head = bf16[320,384]{1,0:T(8,128)(2,1)S(1)} collective-permute-done((bf16[320,384]{1,0:T(8,128)(2,1)S(1)}, bf16[320,384]{1,0:T(8,128)(2,1)S(1)}, u32[]{:S(2)}, u32[]{:S(2)}) %collective-permute-start) | collective-permute-done | bytes 245792 | tf_op jit(solution)/shard_map/ppermute | solution.py:283
  50.5 0.0 copy-done
  50.5 0.0 copy-done.1
  50.5 0.6 first.1
  51.1 7.6 %collective-permute-start.7 = (bf16[2,320,128]{2,1,0:T(8,128)(2,1)S(1)}, bf16[2,320,128]{2,1,0:T(8,128)(2,1)S(1)}, u32[]{:S(2)}, u32[]{:S(2)}) collective-permute-start(bf16[2,320,128]{2,1,0:T(8,128)(2,1)S(1)} %get-tuple-element.23.own), channel_id=1, source_target_pairs={{16,32},{32,16},{48,64},{64,48},{80,96},{96,80},{112,128},{128,112... | collective-permute-start | bytes 491528 | tf_op jit(solution)/shard_map/ppermute | solution.py:291
  58.8 1.9 %collective-permute-start.6 = (bf16[2,320,128]{2,1,0:T(8,128)(2,1)S(1)}, bf16[2,320,128]{2,1,0:T(8,128)(2,1)S(1)}, u32[]{:S(2)}, u32[]{:S(2)}) collective-permute-start(bf16[2,320,128]{2,1,0:T(8,128)(2,1)S(1)} %get-tuple-element.23.own), channel_id=1, source_target_pairs={{0,16},{16,0},{32,48},{48,32},{64,80},{80,64},{96,112},{112,96},{1... | collective-permute-start | bytes 491528 | tf_op jit(solution)/shard_map/ppermute | solution.py:291
  60.7 0.0 copy-done.2
  60.7 0.0 copy-done.3
  60.7 4.8 %merge_local.1.local = bf16[2,320,1920]{2,1,0:T(8,128)(2,1)S(1)} custom-call(s32[1,1,2]{2,1,0:T(1,128)S(1)} %copy-done.1, s32[1,1,2,6]{3,2,1,0:T(2,128)S(1)} %copy-done.2, s32[1,1,2,6]{3,2,1,0:T(2,128)S(1)} %copy-done.3, bf16[1,1,3,320,2240]{4,3,2,1,0:T(8,128)(2,1)} %blocks.3), custom_call_target="tpu_custom_call" | custom-call | tf_op jit(solution)/shard_map/merge_local/pallas_call | solution.py:186
  65.5 0.0 collective-permute-done.7.pair_b
  65.5 0.0 collective-permute-done.6.pair_a
  65.6 0.0 collective-permute-done.5.hi_tail
  65.6 0.0 collective-permute-done.3.lo_tail
  65.6 1.5 %opening.1 = (bf16[2,320,1920]{2,1,0:T(8,128)(2,1)S(1)}, f32[2,320,128]{2,1,0:T(8,128)S(1)}, bf16[2,320,128]{2,1,0:T(8,128)(2,1)S(1)}) custom-call(s32[1,1,2]{2,1,0:T(1,128)S(1)} %copy-done.1, bf16[2,320,1920]{2,1,0:T(8,128)(2,1)S(1)} %merge_local.1.local, bf16[320,384]{1,0:T(8,128)(2,1)S(1)} %collective-permute-done.lower.lo_head, ...), custom_call_target="tpu_custom_call" | custom-call | tf_op jit(solution)/shard_map/opening/pallas_call | solution.py:232
  67.1 3.0 %collective-permute-start.9 = (bf16[2,320,128]{2,1,0:T(8,128)(2,1)S(1)}, bf16[2,320,128]{2,1,0:T(8,128)(2,1)S(1)}, u32[]{:S(2)}, u32[]{:S(2)}) collective-permute-start(bf16[2,320,128]{2,1,0:T(8,128)(2,1)S(1)} %get-tuple-element.26.own), channel_id=1, source_target_pairs={{16,32},{32,16},{48,64},{64,48},{80,96},{96,80},{112,128},{128,112... | collective-permute-start | bytes 491528 | tf_op jit(solution)/shard_map/ppermute | solution.py:291
  70.1 1.9 %collective-permute-start.8 = (bf16[2,320,128]{2,1,0:T(8,128)(2,1)S(1)}, bf16[2,320,128]{2,1,0:T(8,128)(2,1)S(1)}, u32[]{:S(2)}, u32[]{:S(2)}) collective-permute-start(bf16[2,320,128]{2,1,0:T(8,128)(2,1)S(1)} %get-tuple-element.26.own), channel_id=1, source_target_pairs={{0,16},{16,0},{32,48},{48,32},{64,80},{80,64},{96,112},{112,96},{1... | collective-permute-start | bytes 491528 | tf_op jit(solution)/shard_map/ppermute | solution.py:291
  72.1 2.9 %collective-permute-done.9.pair_b = bf16[2,320,128]{2,1,0:T(8,128)(2,1)S(1)} collective-permute-done((bf16[2,320,128]{2,1,0:T(8,128)(2,1)S(1)}, bf16[2,320,128]{2,1,0:T(8,128)(2,1)S(1)}, u32[]{:S(2)}, u32[]{:S(2)}) %collective-permute-start.9) | collective-permute-done | bytes 163872 | tf_op jit(solution)/shard_map/ppermute | solution.py:291
  75.0 0.0 collective-permute-done.8.pair_a
  75.0 0.8 middle.2
  75.8 3.0 %collective-permute-start.11 = (bf16[2,320,128]{2,1,0:T(8,128)(2,1)S(1)}, bf16[2,320,128]{2,1,0:T(8,128)(2,1)S(1)}, u32[]{:S(2)}, u32[]{:S(2)}) collective-permute-start(bf16[2,320,128]{2,1,0:T(8,128)(2,1)S(1)} %get-tuple-element.28.own), channel_id=1, source_target_pairs={{16,32},{32,16},{48,64},{64,48},{80,96},{96,80},{112,128},{128,112... | collective-permute-start | bytes 491528 | tf_op jit(solution)/shard_map/ppermute | solution.py:291
  78.8 1.9 %collective-permute-start.10 = (bf16[2,320,128]{2,1,0:T(8,128)(2,1)S(1)}, bf16[2,320,128]{2,1,0:T(8,128)(2,1)S(1)}, u32[]{:S(2)}, u32[]{:S(2)}) collective-permute-start(bf16[2,320,128]{2,1,0:T(8,128)(2,1)S(1)} %get-tuple-element.28.own), channel_id=1, source_target_pairs={{0,16},{16,0},{32,48},{48,32},{64,80},{80,64},{96,112},{112,96},{1... | collective-permute-start | bytes 491528 | tf_op jit(solution)/shard_map/ppermute | solution.py:291
  80.7 2.9 %collective-permute-done.11.pair_b = bf16[2,320,128]{2,1,0:T(8,128)(2,1)S(1)} collective-permute-done((bf16[2,320,128]{2,1,0:T(8,128)(2,1)S(1)}, bf16[2,320,128]{2,1,0:T(8,128)(2,1)S(1)}, u32[]{:S(2)}, u32[]{:S(2)}) %collective-permute-start.11) | collective-permute-done | bytes 163872 | tf_op jit(solution)/shard_map/ppermute | solution.py:291
  83.6 0.0 collective-permute-done.10.pair_a
  83.6 0.8 middle.3
  84.4 3.0 %collective-permute-start.13 = (bf16[2,320,128]{2,1,0:T(8,128)(2,1)S(1)}, bf16[2,320,128]{2,1,0:T(8,128)(2,1)S(1)}, u32[]{:S(2)}, u32[]{:S(2)}) collective-permute-start(bf16[2,320,128]{2,1,0:T(8,128)(2,1)S(1)} %get-tuple-element.30.own), channel_id=1, source_target_pairs={{16,32},{32,16},{48,64},{64,48},{80,96},{96,80},{112,128},{128,112... | collective-permute-start | bytes 491528 | tf_op jit(solution)/shard_map/ppermute | solution.py:291
  87.5 1.9 %collective-permute-start.12 = (bf16[2,320,128]{2,1,0:T(8,128)(2,1)S(1)}, bf16[2,320,128]{2,1,0:T(8,128)(2,1)S(1)}, u32[]{:S(2)}, u32[]{:S(2)}) collective-permute-start(bf16[2,320,128]{2,1,0:T(8,128)(2,1)S(1)} %get-tuple-element.30.own), channel_id=1, source_target_pairs={{0,16},{16,0},{32,48},{48,32},{64,80},{80,64},{96,112},{112,96},{1... | collective-permute-start | bytes 491528 | tf_op jit(solution)/shard_map/ppermute | solution.py:291
  89.4 2.9 %collective-permute-done.13.pair_b = bf16[2,320,128]{2,1,0:T(8,128)(2,1)S(1)} collective-permute-done((bf16[2,320,128]{2,1,0:T(8,128)(2,1)S(1)}, bf16[2,320,128]{2,1,0:T(8,128)(2,1)S(1)}, u32[]{:S(2)}, u32[]{:S(2)}) %collective-permute-start.13) | collective-permute-done | bytes 163872 | tf_op jit(solution)/shard_map/ppermute | solution.py:291
  92.3 0.0 collective-permute-done.12.pair_a
  92.3 1.5 %closing.1 = f32[1,1,2,320,128]{4,3,2,1,0:T(8,128)} custom-call(bf16[2,320,1920]{2,1,0:T(8,128)(2,1)S(1)} %get-tuple-element.24.merged, bf16[2,320,128]{2,1,0:T(8,128)(2,1)S(1)} %get-tuple-element.22.kept, f32[2,320,128]{2,1,0:T(8,128)S(1)} %get-tuple-element.29.iterate, bf16[2,320,128]{2,1,0:T(8,128)(2,1)S(1)} %get-tuple-element.30.own, ...), custom_call_target="tpu_custom_call" | custom-call | tf_op jit(solution)/shard_map/closing/pallas_call | solution.py:270
Async XLA Ops:
  0.0 14.4 %copy-start.4 = (s32[1,1,2]{2,1,0:T(1,128)S(1)}, s32[1,1,2]{2,1,0:T(1,128)}, u32[]{:S(2)}) copy-start(s32[1,1,2]{2,1,0:T(1,128)} %departure.3) | copy-start | bytes 28
  2.9 47.7 %copy-start = (bf16[1,1,3,320,128]{4,3,2,1,0:T(8,128)(2,1)S(1)}, bf16[1,1,3,320,128]{4,3,2,1,0:T(8,128)(2,1)}, u32[]{:S(2)}) copy-start(bf16[1,1,3,320,128]{4,3,2,1,0:T(8,128)(2,1)} %rhs.3) | copy-start | bytes 737284
  2.9 47.6 %copy-start.1 = (s32[1,1,2]{2,1,0:T(1,128)S(1)}, s32[1,1,2]{2,1,0:T(1,128)}, u32[]{:S(2)}) copy-start(s32[1,1,2]{2,1,0:T(1,128)} %arrival.7) | copy-start | bytes 28
  2.9 7.0 %collective-permute-start.1 = (s32[16]{0:T(128)S(1)}, s32[16]{0:T(128)S(1)}, u32[]{:S(2)}, u32[]{:S(2)}) collective-permute-start(s32[16]{0:T(128)S(1)} %get-tuple-element.19), channel_id=1, source_target_pairs={{1,0},{2,1},{3,2},{4,3},{5,4},{6,5},{7,6},{8,7},{9,8},{10,9},{11,1... | collective-permute-start | bytes 200 | tf_op jit(solution)/shard_map/ppermute | solution.py:283
  7.9 6.4 %collective-permute-start.2 = (s32[16]{0:T(128)S(1)}, s32[16]{0:T(128)S(1)}, u32[]{:S(2)}, u32[]{:S(2)}) collective-permute-start(s32[16]{0:T(128)S(1)} %get-tuple-element.20), channel_id=1, source_target_pairs={{0,1},{1,2},{2,3},{3,4},{4,5},{5,6},{6,7},{7,8},{8,9},{9,10},{10,1... | collective-permute-start | bytes 200 | tf_op jit(solution)/shard_map/ppermute | solution.py:283
  14.4 46.3 %copy-start.2 = (s32[1,1,2,6]{3,2,1,0:T(2,128)S(1)}, s32[1,1,2,6]{3,2,1,0:T(2,128)}, u32[]{:S(2)}) copy-start(s32[1,1,2,6]{3,2,1,0:T(2,128)} %neighbors.3) | copy-start | bytes 148
  14.4 46.3 %copy-start.3 = (s32[1,1,2,6]{3,2,1,0:T(2,128)S(1)}, s32[1,1,2,6]{3,2,1,0:T(2,128)}, u32[]{:S(2)}) copy-start(s32[1,1,2,6]{3,2,1,0:T(2,128)} %orientation.3) | copy-start | bytes 148
  16.4 49.2 %collective-permute-start.5 = (bf16[320,1664]{1,0:T(8,128)(2,1)S(1)}, bf16[320,1664]{1,0:T(8,128)(2,1)S(1)}, u32[]{:S(2)}, u32[]{:S(2)}) collective-permute-start(bf16[320,1664]{1,0:T(8,128)(2,1)S(1)} %merge_tail.1), channel_id=1, source_target_pairs={{1,0},{2,1},{3,2},{4,3},{5,4},{6,5},{7,6},{8,7},{9,8},{10,9},{11,1... | collective-permute-start | bytes 3194888 | tf_op jit(solution)/shard_map/ppermute | solution.py:283
  18.3 47.3 %collective-permute-start.3 = (bf16[320,1664]{1,0:T(8,128)(2,1)S(1)}, bf16[320,1664]{1,0:T(8,128)(2,1)S(1)}, u32[]{:S(2)}, u32[]{:S(2)}) collective-permute-start(bf16[320,1664]{1,0:T(8,128)(2,1)S(1)} %merge_tail.1), channel_id=1, source_target_pairs={{0,1},{1,2},{2,3},{3,4},{4,5},{5,6},{6,7},{7,8},{8,9},{9,10},{10,1... | collective-permute-start | bytes 3194888 | tf_op jit(solution)/shard_map/ppermute | solution.py:283
  21.7 24.8 %collective-permute-start.4 = (bf16[320,384]{1,0:T(8,128)(2,1)S(1)}, bf16[320,384]{1,0:T(8,128)(2,1)S(1)}, u32[]{:S(2)}, u32[]{:S(2)}) collective-permute-start(bf16[320,384]{1,0:T(8,128)(2,1)S(1)} %get-tuple-element.18), channel_id=1, source_target_pairs={{1,0},{2,1},{3,2},{4,3},{5,4},{6,5},{7,6},{8,7},{9,8},{10,9},{11,1... | collective-permute-start | bytes 737288 | tf_op jit(solution)/shard_map/ppermute | solution.py:283
  25.7 24.8 %collective-permute-start = (bf16[320,384]{1,0:T(8,128)(2,1)S(1)}, bf16[320,384]{1,0:T(8,128)(2,1)S(1)}, u32[]{:S(2)}, u32[]{:S(2)}) collective-permute-start(bf16[320,384]{1,0:T(8,128)(2,1)S(1)} %get-tuple-element.18), channel_id=1, source_target_pairs={{0,1},{1,2},{2,3},{3,4},{4,5},{5,6},{6,7},{7,8},{8,9},{9,10},{10,1... | collective-permute-start | bytes 737288 | tf_op jit(solution)/shard_map/ppermute | solution.py:283
  51.1 14.4 %collective-permute-start.7 = (bf16[2,320,128]{2,1,0:T(8,128)(2,1)S(1)}, bf16[2,320,128]{2,1,0:T(8,128)(2,1)S(1)}, u32[]{:S(2)}, u32[]{:S(2)}) collective-permute-start(bf16[2,320,128]{2,1,0:T(8,128)(2,1)S(1)} %get-tuple-element.23.own), channel_id=1, source_target_pairs={{16,32},{32,16},{48,64},{64,48},{80,96},{96,80},{112,128},{128,112... | collective-permute-start | bytes 491528 | tf_op jit(solution)/shard_map/ppermute | solution.py:291
  58.8 6.8 %collective-permute-start.6 = (bf16[2,320,128]{2,1,0:T(8,128)(2,1)S(1)}, bf16[2,320,128]{2,1,0:T(8,128)(2,1)S(1)}, u32[]{:S(2)}, u32[]{:S(2)}) collective-permute-start(bf16[2,320,128]{2,1,0:T(8,128)(2,1)S(1)} %get-tuple-element.23.own), channel_id=1, source_target_pairs={{0,16},{16,0},{32,48},{48,32},{64,80},{80,64},{96,112},{112,96},{1... | collective-permute-start | bytes 491528 | tf_op jit(solution)/shard_map/ppermute | solution.py:291
  67.1 7.8 %collective-permute-start.9 = (bf16[2,320,128]{2,1,0:T(8,128)(2,1)S(1)}, bf16[2,320,128]{2,1,0:T(8,128)(2,1)S(1)}, u32[]{:S(2)}, u32[]{:S(2)}) collective-permute-start(bf16[2,320,128]{2,1,0:T(8,128)(2,1)S(1)} %get-tuple-element.26.own), channel_id=1, source_target_pairs={{16,32},{32,16},{48,64},{64,48},{80,96},{96,80},{112,128},{128,112... | collective-permute-start | bytes 491528 | tf_op jit(solution)/shard_map/ppermute | solution.py:291
  70.1 4.8 %collective-permute-start.8 = (bf16[2,320,128]{2,1,0:T(8,128)(2,1)S(1)}, bf16[2,320,128]{2,1,0:T(8,128)(2,1)S(1)}, u32[]{:S(2)}, u32[]{:S(2)}) collective-permute-start(bf16[2,320,128]{2,1,0:T(8,128)(2,1)S(1)} %get-tuple-element.26.own), channel_id=1, source_target_pairs={{0,16},{16,0},{32,48},{48,32},{64,80},{80,64},{96,112},{112,96},{1... | collective-permute-start | bytes 491528 | tf_op jit(solution)/shard_map/ppermute | solution.py:291
  75.8 7.8 %collective-permute-start.11 = (bf16[2,320,128]{2,1,0:T(8,128)(2,1)S(1)}, bf16[2,320,128]{2,1,0:T(8,128)(2,1)S(1)}, u32[]{:S(2)}, u32[]{:S(2)}) collective-permute-start(bf16[2,320,128]{2,1,0:T(8,128)(2,1)S(1)} %get-tuple-element.28.own), channel_id=1, source_target_pairs={{16,32},{32,16},{48,64},{64,48},{80,96},{96,80},{112,128},{128,112... | collective-permute-start | bytes 491528 | tf_op jit(solution)/shard_map/ppermute | solution.py:291
  78.8 4.8 %collective-permute-start.10 = (bf16[2,320,128]{2,1,0:T(8,128)(2,1)S(1)}, bf16[2,320,128]{2,1,0:T(8,128)(2,1)S(1)}, u32[]{:S(2)}, u32[]{:S(2)}) collective-permute-start(bf16[2,320,128]{2,1,0:T(8,128)(2,1)S(1)} %get-tuple-element.28.own), channel_id=1, source_target_pairs={{0,16},{16,0},{32,48},{48,32},{64,80},{80,64},{96,112},{112,96},{1... | collective-permute-start | bytes 491528 | tf_op jit(solution)/shard_map/ppermute | solution.py:291
  84.4 7.8 %collective-permute-start.13 = (bf16[2,320,128]{2,1,0:T(8,128)(2,1)S(1)}, bf16[2,320,128]{2,1,0:T(8,128)(2,1)S(1)}, u32[]{:S(2)}, u32[]{:S(2)}) collective-permute-start(bf16[2,320,128]{2,1,0:T(8,128)(2,1)S(1)} %get-tuple-element.30.own), channel_id=1, source_target_pairs={{16,32},{32,16},{48,64},{64,48},{80,96},{96,80},{112,128},{128,112... | collective-permute-start | bytes 491528 | tf_op jit(solution)/shard_map/ppermute | solution.py:291
  87.5 4.8 %collective-permute-start.12 = (bf16[2,320,128]{2,1,0:T(8,128)(2,1)S(1)}, bf16[2,320,128]{2,1,0:T(8,128)(2,1)S(1)}, u32[]{:S(2)}, u32[]{:S(2)}) collective-permute-start(bf16[2,320,128]{2,1,0:T(8,128)(2,1)S(1)} %get-tuple-element.30.own), channel_id=1, source_target_pairs={{0,16},{16,0},{32,48},{48,32},{64,80},{80,64},{96,112},{112,96},{1... | collective-permute-start | bytes 491528 | tf_op jit(solution)/shard_map/ppermute | solution.py:291

commit v2 on v1

v2 whole, which is shorter than its diff:
```python
import jax
import jax.numpy as jnp
from jax import lax
from jax.experimental import pallas as pl
from jax.experimental.pallas import tpu as pltpu
from jax.sharding import PartitionSpec as P


DOF = 320
FACES = 6
RHS = 128
KEPT = 2
ITERS = 4
RELAXATION = 0.7
WIDE = 7 * DOF
TILE = 128
SLOTS = 6
MERGED = SLOTS * DOF
TILES = MERGED // TILE
HEAD = 2
SPAN = 3
LAST = DOF * FACES


def vmem(shape, dtype):
    return pltpu.VMEM(shape, dtype)


def near(*arrays):
    return tuple(pltpu.with_memory_space_constraint(array, pltpu.VMEM) for array in arrays)


def far(*arrays):
    return tuple(pltpu.with_memory_space_constraint(array, pltpu.HBM) for array in arrays)


PARAMS = pltpu.CompilerParams(vmem_limit_bytes=20 * 2**20)

SMEM_SPEC = pl.BlockSpec(memory_space=pltpu.SMEM)
VMEM_SPEC = pl.BlockSpec(memory_space=pltpu.VMEM)
ANY_SPEC = pl.BlockSpec(memory_space=pl.ANY)


def turned_select(start, n, k, parity):
    shift = start % TILE
    layer = n // 2
    first = jnp.where(parity == 0, layer == 2, layer == 0)
    slot = jnp.where(layer == 1, 1, jnp.where(first, 2, 4) + n % 2)
    place = DOF * slot
    tile = place // TILE
    column = lax.broadcasted_iota(jnp.int32, (1, SPAN * TILE), 1) - (place - tile * TILE)
    a = (column // 16) % 4
    b = (column // 4) % 4
    source_a = jnp.where(k == 0, a, jnp.where(k == 1, 3 - b, jnp.where(k == 2, 3 - a, b)))
    source_b = jnp.where(k == 0, b, jnp.where(k == 1, a, jnp.where(k == 2, 3 - b, 3 - a)))
    source = shift + (column // 64) * 64 + source_a * 16 + source_b * 4 + column % 4
    source = jnp.where((column >= 0) & (column < DOF), source, -1)
    rows = lax.broadcasted_iota(jnp.int32, (DOF + shift, SPAN * TILE), 0)
    return tile, jnp.where(rows == source, 1.0, 0.0).astype(jnp.bfloat16)


def add_faces(faces, columns, neighbor, turn, parity, acc_ref):
    for face in faces:
        start = DOF * (face + 1)
        tile, select = turned_select(start, neighbor(face), turn(face), parity)
        base = start - start % TILE
        moved = jnp.dot(columns(base, start + DOF), select, preferred_element_type=jnp.float32)
        for part in range(SPAN):
            acc_ref[tile + part] += moved[:, part * TILE : (part + 1) * TILE]


def put_own(columns, acc_ref):
    lane = lax.broadcasted_iota(jnp.int32, (DOF, TILE), 1)
    for tile in range(TILES):
        if tile <= HEAD:
            acc_ref[tile] = columns(tile * TILE, (tile + 1) * TILE).astype(jnp.float32)
        else:
            acc_ref[tile] = jnp.zeros((DOF, TILE), jnp.float32)
    acc_ref[HEAD] = jnp.where(lane < DOF - HEAD * TILE, acc_ref[HEAD], 0.0)


def pick_kernel(departure, blocks, rhs, head, middle, last, row, sems):
    slot = jnp.maximum(jnp.maximum(departure[0, 0, 0], departure[0, 0, 1]), 0)
    whole = pltpu.make_async_copy(blocks.at[0, 0, slot], row, sems.at[0])
    side = pltpu.make_async_copy(rhs.at[0, 0, slot], head.at[:, 0:RHS], sems.at[1])
    whole.start()
    side.start()
    whole.wait()
    side.wait()
    head[:, RHS:] = row[:, 0 : HEAD * TILE]
    middle[...] = row[:, HEAD * TILE : LAST]
    last[...] = row[:, LAST:]


def pick(departure, blocks, rhs):
    return pl.pallas_call(
        pick_kernel,
        in_specs=[SMEM_SPEC] + [ANY_SPEC] * 2,
        out_specs=[VMEM_SPEC] * 3,
        out_shape=[
            vmem((DOF, RHS + HEAD * TILE), jnp.bfloat16),
            vmem((DOF, LAST - HEAD * TILE), jnp.bfloat16),
            vmem((DOF, DOF), jnp.bfloat16),
        ],
        scratch_shapes=[pltpu.VMEM((DOF, WIDE), jnp.bfloat16), pltpu.SemaphoreType.DMA((2,))],
        compiler_params=PARAMS,
        name="pick",
    )(*far(departure, blocks, rhs))


def first_kernel(arrival, rhs, lower, upper, kept, rounded):
    for q in range(KEPT):
        source = arrival[0, 0, q]

        @pl.when(source < 3)
        def _():
            kept[q] = rhs[0, 0, jnp.clip(source, 0, 2)]

        @pl.when(source == 3)
        def _():
            kept[q] = lower[:, 0:RHS]

        @pl.when(source == 4)
        def _():
            kept[q] = upper[:, 0:RHS]

        rounded[q] = (RELAXATION * kept[q].astype(jnp.float32)).astype(jnp.bfloat16)


def first(arrival, rhs, lower, upper):
    pair = vmem((KEPT, DOF, RHS), jnp.bfloat16)
    return pl.pallas_call(
        first_kernel,
        in_specs=[SMEM_SPEC] + [VMEM_SPEC] * 3,
        out_specs=[VMEM_SPEC] * 2,
        out_shape=[pair, pair],
        compiler_params=PARAMS,
        name="first",
    )(arrival, *near(rhs, lower, upper))


def local_kernel(arrival, neighbors, orientation, blocks, merged, rows, acc, sems):
    parity = lax.axis_index("gx") % 2
    copies = [
        pltpu.make_async_copy(blocks.at[0, 0, jnp.clip(arrival[0, 0, q], 0, 2)], rows.at[q], sems.at[q])
        for q in range(KEPT)
    ]
    for copy in copies:
        copy.start()
    for q in range(KEPT):
        copies[q].wait()

        @pl.when(arrival[0, 0, q] < 3)
        def _():
            columns = lambda low, high: rows[q, :, low:high]
            put_own(columns, acc)
            neighbor = lambda face: neighbors[0, 0, q, face]
            turn = lambda face: orientation[0, 0, q, face]
            add_faces(range(FACES), columns, neighbor, turn, parity, acc)
            for tile in range(TILES):
                merged[q, :, tile * TILE : (tile + 1) * TILE] = acc[tile].astype(jnp.bfloat16)


def merged_local(arrival, neighbors, orientation, blocks):
    return pl.pallas_call(
        local_kernel,
        in_specs=[SMEM_SPEC] * 3 + [ANY_SPEC],
        out_specs=VMEM_SPEC,
        out_shape=vmem((KEPT, DOF, MERGED), jnp.bfloat16),
        scratch_shapes=[
            pltpu.VMEM((KEPT, DOF, WIDE), jnp.bfloat16),
            pltpu.VMEM((TILES, DOF, TILE), jnp.float32),
            pltpu.SemaphoreType.DMA((KEPT,)),
        ],
        compiler_params=PARAMS,
        name="merge_local",
    )(arrival, neighbors, orientation, *far(blocks))


def arrived_kernel(
    arrival, neighbors, orientation, local, lo_head, lo_middle, hi_head, hi_middle, merged, acc
):
    del local
    parity = lax.axis_index("gx") % 2
    for q in range(KEPT):
        for code, head, middle in ((3, lo_head, lo_middle), (4, hi_head, hi_middle)):

            @pl.when(arrival[0, 0, q] == code)
            def _():
                def columns(low, high):
                    if high <= HEAD * TILE:
                        return head[:, RHS + low : RHS + high]
                    return middle[:, low - HEAD * TILE : high - HEAD * TILE]

                put_own(columns, acc.at[q])
                neighbor = lambda face: neighbors[0, 0, q, face]
                turn = lambda face: orientation[0, 0, q, face]
                add_faces(range(FACES - 1), columns, neighbor, turn, parity, acc.at[q])
                for tile in range(TILES):
                    merged[q, :, tile * TILE : (tile + 1) * TILE] = acc[q, tile].astype(jnp.bfloat16)


def merged_arrived(arrival, neighbors, orientation, local, lo_head, lo_middle, hi_head, hi_middle):
    return pl.pallas_call(
        arrived_kernel,
        in_specs=[SMEM_SPEC] * 3 + [VMEM_SPEC] * 5,
        out_specs=[VMEM_SPEC] * 2,
        out_shape=[
            vmem((KEPT, DOF, MERGED), jnp.bfloat16),
            vmem((KEPT, TILES, DOF, TILE), jnp.float32),
        ],
        input_output_aliases={3: 0},
        compiler_params=PARAMS,
        name="merge_arrived",
    )(arrival, neighbors, orientation, *near(local, lo_head, lo_middle, hi_head, hi_middle))


def applied_rows(merged, own, pair_a, pair_b):
    far = jnp.concatenate([pair_a[0], pair_a[1], pair_b[0], pair_b[1]], axis=0)
    for q in range(KEPT):
        near = jnp.concatenate([own[q], own[1 - q]], axis=0)
        applied = jnp.dot(merged[q, :, 0 : 2 * DOF], near, preferred_element_type=jnp.float32)
        applied += jnp.dot(merged[q, :, 2 * DOF :], far, preferred_element_type=jnp.float32)
        yield q, applied


def opening_kernel(
    arrival, neighbors, orientation, partial, acc, lo_last, hi_last, kept, own, pair_a, pair_b, merged, iterate, rounded
):
    del partial
    parity = lax.axis_index("gx") % 2
    for q in range(KEPT):
        for code, last in ((3, lo_last), (4, hi_last)):

            @pl.when(arrival[0, 0, q] == code)
            def _():
                face = FACES - 1
                tile, select = turned_select(LAST, neighbors[0, 0, q, face], orientation[0, 0, q, face], parity)
                moved = jnp.dot(last[...], select, preferred_element_type=jnp.float32)
                for part in range(SPAN):
                    total = acc[q, tile + part] + moved[:, part * TILE : (part + 1) * TILE]
                    place = pl.multiple_of((tile + part) * TILE, TILE)
                    merged[q, :, pl.ds(place, TILE)] = total.astype(jnp.bfloat16)

    for q, applied in applied_rows(merged, own, pair_a, pair_b):
        side = kept[q].astype(jnp.float32)
        value = RELAXATION * side + RELAXATION * (side - applied)
        iterate[q] = value
        rounded[q] = value.astype(jnp.bfloat16)


def opening(arrival, neighbors, orientation, partial, acc, lo_last, hi_last, kept, own, pair_a, pair_b):
    return pl.pallas_call(
        opening_kernel,
        in_specs=[SMEM_SPEC] * 3 + [VMEM_SPEC] * 8,
        out_specs=[VMEM_SPEC] * 3,
        out_shape=[
            vmem((KEPT, DOF, MERGED), jnp.bfloat16),
            vmem((KEPT, DOF, RHS), jnp.float32),
            vmem((KEPT, DOF, RHS), jnp.bfloat16),
        ],
        input_output_aliases={3: 0},
        compiler_params=PARAMS,
        name="opening",
    )(arrival, neighbors, orientation, *near(partial, acc, lo_last, hi_last, kept, own, pair_a, pair_b))


def middle_kernel(merged, kept, iterate, own, pair_a, pair_b, iterate_out, rounded):
    for q, applied in applied_rows(merged, own, pair_a, pair_b):
        value = iterate[q] + RELAXATION * (kept[q].astype(jnp.float32) - applied)
        iterate_out[q] = value
        rounded[q] = value.astype(jnp.bfloat16)


def middle(merged, kept, iterate, own, pair_a, pair_b):
    return pl.pallas_call(
        middle_kernel,
        in_specs=[VMEM_SPEC] * 6,
        out_specs=[VMEM_SPEC] * 2,
        out_shape=[vmem((KEPT, DOF, RHS), jnp.float32), vmem((KEPT, DOF, RHS), jnp.bfloat16)],
        compiler_params=PARAMS,
        name="middle",
    )(*near(merged, kept, iterate, own, pair_a, pair_b))


def closing_kernel(merged, kept, iterate, own, pair_a, pair_b, smoothed):
    for q, applied in applied_rows(merged, own, pair_a, pair_b):
        smoothed[0, 0, q] = iterate[q] + RELAXATION * (kept[q].astype(jnp.float32) - applied)


def closing(merged, kept, iterate, own, pair_a, pair_b):
    return pl.pallas_call(
        closing_kernel,
        in_specs=[VMEM_SPEC] * 6,
        out_specs=VMEM_SPEC,
        out_shape=jax.ShapeDtypeStruct((1, 1, KEPT, DOF, RHS), jnp.float32),
        compiler_params=PARAMS,
        name="closing",
    )(*near(merged, kept, iterate, own, pair_a, pair_b))


def shifted(value, axis, steps):
    count = lax.axis_size(axis)
    leading, last = (max(0, -steps), min(count, count - steps))
    return lax.ppermute(value, axis, [(source, source + steps) for source in range(leading, last)])


def swapped(value, axis, start):
    count = lax.axis_size(axis)
    pairs = []
    for low in range(start, count - 1, 2):
        pairs += [(low, low + 1), (low + 1, low)]
    return lax.ppermute(value, axis, pairs)


def halo(rounded):
    pair_b = swapped(rounded, "gx", 1)
    pair_a = swapped(rounded, "gx", 0)
    return pair_a, pair_b


def both_ways(value):
    lower = shifted(value, "gy", 1)
    upper = shifted(value, "gy", -1)
    return lower, upper


def shards(blocks, right_side, departure, arrival, neighbors, orientation):
    head, middle_columns, last = pick(departure, blocks, right_side)
    lo_head, hi_head = both_ways(head)
    lo_middle, hi_middle = both_ways(middle_columns)
    lo_last, hi_last = both_ways(last)
    kept, own = first(arrival, right_side, lo_head, hi_head)
    pair_a, pair_b = halo(own)
    local = merged_local(arrival, neighbors, orientation, blocks)
    partial, acc = merged_arrived(
        arrival, neighbors, orientation, local, lo_head, lo_middle, hi_head, hi_middle
    )
    merged, iterate, own = opening(
        arrival, neighbors, orientation, partial, acc, lo_last, hi_last, kept, own, pair_a, pair_b
    )
    for _ in range(1, ITERS - 1):
        pair_a, pair_b = halo(own)
        iterate, own = middle(merged, kept, iterate, own, pair_a, pair_b)
    pair_a, pair_b = halo(own)
    return closing(merged, kept, iterate, own, pair_a, pair_b)


def solution(mesh):
    in_specs = (
        P("gx", "gy", None, None, None),
        P("gx", "gy", None, None, None),
        P("gx", "gy", None),
        P("gx", "gy", None),
        P("gx", "gy", None, None),
        P("gx", "gy", None, None),
    )
    out_specs = P("gx", "gy", None, None, None)
    return jax.shard_map(shards, mesh=mesh, in_specs=in_specs, out_specs=out_specs, check_vma=False)
```

time: 94.4 us -> 89.1 us (0.944)
  the two profiles are of different devices: /device:TPU:231 before, /device:TPU:103 now
where the time goes in v2:
time: 89.1 us; the launch traced here: 88.6 us
  starting transfers between devices  46 us (52%)
  waiting for transfers between devices  29.2 us (33%)
  Pallas kernels  13.1 us (15%)
    ppermute x8, starting transfers between devices, swapped(): return lax.ppermute(value, axis, pairs)  26.5 us
    ppermute x6, starting transfers between devices, shifted(): lax.ppermute(value, axis, [(source, source + steps) for source in range(l...  19.5 us
    ppermute x6, waiting for transfers between devices, shifted(): lax.ppermute(value, axis, [(source, source + steps) for source in range(l...  16.9 us
    ppermute x8, waiting for transfers between devices, swapped(): return lax.ppermute(value, axis, pairs)  12.2 us
    pallas_call x1, Pallas kernels, merged_local(): pl.pallas_call(local_kernel, in_specs=[SMEM_SPEC] * 3 + [ANY_SPEC], out_s...  3.41 us
    pallas_call x1, Pallas kernels, pick(): pl.pallas_call(pick_kernel, in_specs=[SMEM_SPEC] + [ANY_SPEC] * 2, out_sp...  2.3 us
    pallas_call x1, Pallas kernels, merged_arrived(): pl.pallas_call(arrived_kernel, in_specs=[SMEM_SPEC] * 3 + [VMEM_SPEC] * 5...  1.86 us
  transfers between devices with their start and end apart: 14, of which 4 were waited for; matrix products, arithmetic and copies ran while one was open for 0% of the time, Pallas kernels for 7%

profile of v2, /device:TPU:103, one launch (start us, length us, event | category | flops | bytes accessed | tf_op | source)
XLA Modules:
  0.0 88.6 jit_solution(9501923377627382180)
XLA Ops:
  0.0 0.0 copy-start
  0.0 0.0 copy-start.3
  0.0 0.0 copy-start.1
  0.0 0.0 copy-start.2
  0.0 2.3 %pick.1 = (bf16[320,384]{1,0:T(8,128)(2,1)S(1)}, bf16[320,1664]{1,0:T(8,128)(2,1)S(1)}, bf16[320,320]{1,0:T(8,128)(2,1)S(1)}) custom-call(s32[1,1,2]{2,1,0:T(1,128)} %departure.1, bf16[1,1,3,320,2240]{4,3,2,1,0:T(8,128)(2,1)} %blocks.3, bf16[1,1,3,320,128]{4,3,2,1,0:T(8,128)(2,1)} %rhs.3), custom_call_target="tpu_custom_call" | custom-call | tf_op jit(solution)/shard_map/pick/pallas_call | solution.py:96
  2.3 3.2 %collective-permute-start.1 = (bf16[320,1664]{1,0:T(8,128)(2,1)S(1)}, bf16[320,1664]{1,0:T(8,128)(2,1)S(1)}, u32[]{:S(2)}, u32[]{:S(2)}) collective-permute-start(bf16[320,1664]{1,0:T(8,128)(2,1)S(1)} %get-tuple-element.20), channel_id=1, source_target_pairs={{0,1},{1,2},{2,3},{3,4},{4,5},{5,6},{6,7},{7,8},{8,9},{9,10},{10,1... | collective-permute-start | bytes 3194888 | tf_op jit(solution)/shard_map/ppermute | solution.py:305
  5.5 4.2 %collective-permute-start.3 = (bf16[320,1664]{1,0:T(8,128)(2,1)S(1)}, bf16[320,1664]{1,0:T(8,128)(2,1)S(1)}, u32[]{:S(2)}, u32[]{:S(2)}) collective-permute-start(bf16[320,1664]{1,0:T(8,128)(2,1)S(1)} %get-tuple-element.20), channel_id=1, source_target_pairs={{1,0},{2,1},{3,2},{4,3},{5,4},{6,5},{7,6},{8,7},{9,8},{10,9},{11,1... | collective-permute-start | bytes 3194888 | tf_op jit(solution)/shard_map/ppermute | solution.py:305
  9.7 1.9 %collective-permute-start = (bf16[320,384]{1,0:T(8,128)(2,1)S(1)}, bf16[320,384]{1,0:T(8,128)(2,1)S(1)}, u32[]{:S(2)}, u32[]{:S(2)}) collective-permute-start(bf16[320,384]{1,0:T(8,128)(2,1)S(1)} %get-tuple-element.19), channel_id=1, source_target_pairs={{0,1},{1,2},{2,3},{3,4},{4,5},{5,6},{6,7},{7,8},{8,9},{9,10},{10,1... | collective-permute-start | bytes 737288 | tf_op jit(solution)/shard_map/ppermute | solution.py:305
  11.7 5.5 %collective-permute-start.2 = (bf16[320,384]{1,0:T(8,128)(2,1)S(1)}, bf16[320,384]{1,0:T(8,128)(2,1)S(1)}, u32[]{:S(2)}, u32[]{:S(2)}) collective-permute-start(bf16[320,384]{1,0:T(8,128)(2,1)S(1)} %get-tuple-element.19), channel_id=1, source_target_pairs={{1,0},{2,1},{3,2},{4,3},{5,4},{6,5},{7,6},{8,7},{9,8},{10,9},{11,1... | collective-permute-start | bytes 737288 | tf_op jit(solution)/shard_map/ppermute | solution.py:305
  17.1 1.9 %collective-permute-start.4 = (bf16[320,320]{1,0:T(8,128)(2,1)S(1)}, bf16[320,320]{1,0:T(8,128)(2,1)S(1)}, u32[]{:S(2)}, u32[]{:S(2)}) collective-permute-start(bf16[320,320]{1,0:T(8,128)(2,1)S(1)} %get-tuple-element.23), channel_id=1, source_target_pairs={{0,1},{1,2},{2,3},{3,4},{4,5},{5,6},{6,7},{7,8},{8,9},{9,10},{10,1... | collective-permute-start | bytes 614408 | tf_op jit(solution)/shard_map/ppermute | solution.py:305
  19.1 16.9 %collective-permute-done.lo_head.lower = bf16[320,384]{1,0:T(8,128)(2,1)S(1)} collective-permute-done((bf16[320,384]{1,0:T(8,128)(2,1)S(1)}, bf16[320,384]{1,0:T(8,128)(2,1)S(1)}, u32[]{:S(2)}, u32[]{:S(2)}) %collective-permute-start) | collective-permute-done | bytes 245792 | tf_op jit(solution)/shard_map/ppermute | solution.py:305
  36.0 2.8 %collective-permute-start.5 = (bf16[320,320]{1,0:T(8,128)(2,1)S(1)}, bf16[320,320]{1,0:T(8,128)(2,1)S(1)}, u32[]{:S(2)}, u32[]{:S(2)}) collective-permute-start(bf16[320,320]{1,0:T(8,128)(2,1)S(1)} %get-tuple-element.23), channel_id=1, source_target_pairs={{1,0},{2,1},{3,2},{4,3},{5,4},{6,5},{7,6},{8,7},{9,8},{10,9},{11,1... | collective-permute-start | bytes 614408 | tf_op jit(solution)/shard_map/ppermute | solution.py:305
  38.8 0.0 collective-permute-done.2.hi_head.upper
  38.8 0.0 copy-done
  38.8 0.0 copy-done.3
  38.8 0.6 first.1
  39.4 4.8 %collective-permute-start.6 = (bf16[2,320,128]{2,1,0:T(8,128)(2,1)S(1)}, bf16[2,320,128]{2,1,0:T(8,128)(2,1)S(1)}, u32[]{:S(2)}, u32[]{:S(2)}) collective-permute-start(bf16[2,320,128]{2,1,0:T(8,128)(2,1)S(1)} %get-tuple-element.25.own), channel_id=1, source_target_pairs={{0,16},{16,0},{32,48},{48,32},{64,80},{80,64},{96,112},{112,96},{1... | collective-permute-start | bytes 491528 | tf_op jit(solution)/shard_map/ppermute | solution.py:313
  44.3 0.0 collective-permute-done.1.lo_middle
  44.3 4.7 %collective-permute-start.7 = (bf16[2,320,128]{2,1,0:T(8,128)(2,1)S(1)}, bf16[2,320,128]{2,1,0:T(8,128)(2,1)S(1)}, u32[]{:S(2)}, u32[]{:S(2)}) collective-permute-start(bf16[2,320,128]{2,1,0:T(8,128)(2,1)S(1)} %get-tuple-element.25.own), channel_id=1, source_target_pairs={{16,32},{32,16},{48,64},{64,48},{80,96},{96,80},{112,128},{128,112... | collective-permute-start | bytes 491528 | tf_op jit(solution)/shard_map/ppermute | solution.py:313
  49.0 0.0 copy-done.1
  49.0 0.0 copy-done.2
  49.0 3.4 %merge_local.1.local = bf16[2,320,1920]{2,1,0:T(8,128)(2,1)S(1)} custom-call(s32[1,1,2]{2,1,0:T(1,128)S(1)} %copy-done.3, s32[1,1,2,6]{3,2,1,0:T(2,128)S(1)} %copy-done.1, s32[1,1,2,6]{3,2,1,0:T(2,128)S(1)} %copy-done.2, bf16[1,1,3,320,2240]{4,3,2,1,0:T(8,128)(2,1)} %blocks.3), custom_call_target="tpu_custom_call" | custom-call | tf_op jit(solution)/shard_map/merge_local/pallas_call | solution.py:165
  52.4 0.0 collective-permute-done.3.hi_middle
  52.4 1.9 %merge_arrived.1 = (bf16[2,320,1920]{2,1,0:T(8,128)(2,1)S(1)}, f32[2,15,320,128]{3,2,1,0:T(8,128)S(1)}) custom-call(s32[1,1,2]{2,1,0:T(1,128)S(1)} %copy-done.3, s32[1,1,2,6]{3,2,1,0:T(2,128)S(1)} %copy-done.1, s32[1,1,2,6]{3,2,1,0:T(2,128)S(1)} %copy-done.2, bf16[2,320,1920]{2,1,0:T(8,128)(2,1)S(1)} %merge_local.1.local, ...), custom_call_target="tpu_custom_call", output_to_operand_aliasing={{0}: (3, {})} | custom-call | tf_op jit(solution)/shard_map/merge_arrived/pallas_call | solution.py:204
  54.3 0.0 collective-permute-done.4.lo_last
  54.3 0.0 collective-permute-done.5.hi_last
  54.3 0.0 collective-permute-done.6.pair_a
  54.3 0.0 collective-permute-done.7.pair_b
  54.3 1.8 %opening.1 = (bf16[2,320,1920]{2,1,0:T(8,128)(2,1)S(1)}, f32[2,320,128]{2,1,0:T(8,128)S(1)}, bf16[2,320,128]{2,1,0:T(8,128)(2,1)S(1)}) custom-call(s32[1,1,2]{2,1,0:T(1,128)S(1)} %copy-done.3, s32[1,1,2,6]{3,2,1,0:T(2,128)S(1)} %copy-done.1, s32[1,1,2,6]{3,2,1,0:T(2,128)S(1)} %copy-done.2, ...), custom_call_target="tpu_custom_call", output_to_operand_aliasing={{0}: (3, {})} | custom-call | tf_op jit(solution)/shard_map/opening/pallas_call | solution.py:253
  56.1 1.9 %collective-permute-start.8 = (bf16[2,320,128]{2,1,0:T(8,128)(2,1)S(1)}, bf16[2,320,128]{2,1,0:T(8,128)(2,1)S(1)}, u32[]{:S(2)}, u32[]{:S(2)}) collective-permute-start(bf16[2,320,128]{2,1,0:T(8,128)(2,1)S(1)} %get-tuple-element.28.own), channel_id=1, source_target_pairs={{0,16},{16,0},{32,48},{48,32},{64,80},{80,64},{96,112},{112,96},{1... | collective-permute-start | bytes 491528 | tf_op jit(solution)/shard_map/ppermute | solution.py:313
  58.0 3.8 %collective-permute-start.9 = (bf16[2,320,128]{2,1,0:T(8,128)(2,1)S(1)}, bf16[2,320,128]{2,1,0:T(8,128)(2,1)S(1)}, u32[]{:S(2)}, u32[]{:S(2)}) collective-permute-start(bf16[2,320,128]{2,1,0:T(8,128)(2,1)S(1)} %get-tuple-element.28.own), channel_id=1, source_target_pairs={{16,32},{32,16},{48,64},{64,48},{80,96},{96,80},{112,128},{128,112... | collective-permute-start | bytes 491528 | tf_op jit(solution)/shard_map/ppermute | solution.py:313
  61.8 0.0 collective-permute-done.8.pair_a
  61.8 4.1 %collective-permute-done.9.pair_b = bf16[2,320,128]{2,1,0:T(8,128)(2,1)S(1)} collective-permute-done((bf16[2,320,128]{2,1,0:T(8,128)(2,1)S(1)}, bf16[2,320,128]{2,1,0:T(8,128)(2,1)S(1)}, u32[]{:S(2)}, u32[]{:S(2)}) %collective-permute-start.9) | collective-permute-done | bytes 163872 | tf_op jit(solution)/shard_map/ppermute | solution.py:313
  65.9 0.8 middle.2
  66.7 1.9 %collective-permute-start.10 = (bf16[2,320,128]{2,1,0:T(8,128)(2,1)S(1)}, bf16[2,320,128]{2,1,0:T(8,128)(2,1)S(1)}, u32[]{:S(2)}, u32[]{:S(2)}) collective-permute-start(bf16[2,320,128]{2,1,0:T(8,128)(2,1)S(1)} %get-tuple-element.30.own), channel_id=1, source_target_pairs={{0,16},{16,0},{32,48},{48,32},{64,80},{80,64},{96,112},{112,96},{1... | collective-permute-start | bytes 491528 | tf_op jit(solution)/shard_map/ppermute | solution.py:313
  68.6 3.8 %collective-permute-start.11 = (bf16[2,320,128]{2,1,0:T(8,128)(2,1)S(1)}, bf16[2,320,128]{2,1,0:T(8,128)(2,1)S(1)}, u32[]{:S(2)}, u32[]{:S(2)}) collective-permute-start(bf16[2,320,128]{2,1,0:T(8,128)(2,1)S(1)} %get-tuple-element.30.own), channel_id=1, source_target_pairs={{16,32},{32,16},{48,64},{64,48},{80,96},{96,80},{112,128},{128,112... | collective-permute-start | bytes 491528 | tf_op jit(solution)/shard_map/ppermute | solution.py:313
  72.4 0.0 collective-permute-done.10.pair_a
  72.4 4.1 %collective-permute-done.11.pair_b = bf16[2,320,128]{2,1,0:T(8,128)(2,1)S(1)} collective-permute-done((bf16[2,320,128]{2,1,0:T(8,128)(2,1)S(1)}, bf16[2,320,128]{2,1,0:T(8,128)(2,1)S(1)}, u32[]{:S(2)}, u32[]{:S(2)}) %collective-permute-start.11) | collective-permute-done | bytes 163872 | tf_op jit(solution)/shard_map/ppermute | solution.py:313
  76.5 0.8 middle.3
  77.3 1.9 %collective-permute-start.12 = (bf16[2,320,128]{2,1,0:T(8,128)(2,1)S(1)}, bf16[2,320,128]{2,1,0:T(8,128)(2,1)S(1)}, u32[]{:S(2)}, u32[]{:S(2)}) collective-permute-start(bf16[2,320,128]{2,1,0:T(8,128)(2,1)S(1)} %get-tuple-element.32.own), channel_id=1, source_target_pairs={{0,16},{16,0},{32,48},{48,32},{64,80},{80,64},{96,112},{112,96},{1... | collective-permute-start | bytes 491528 | tf_op jit(solution)/shard_map/ppermute | solution.py:313
  79.2 3.8 %collective-permute-start.13 = (bf16[2,320,128]{2,1,0:T(8,128)(2,1)S(1)}, bf16[2,320,128]{2,1,0:T(8,128)(2,1)S(1)}, u32[]{:S(2)}, u32[]{:S(2)}) collective-permute-start(bf16[2,320,128]{2,1,0:T(8,128)(2,1)S(1)} %get-tuple-element.32.own), channel_id=1, source_target_pairs={{16,32},{32,16},{48,64},{64,48},{80,96},{96,80},{112,128},{128,112... | collective-permute-start | bytes 491528 | tf_op jit(solution)/shard_map/ppermute | solution.py:313
  83.0 0.0 collective-permute-done.12.pair_a
  83.0 4.1 %collective-permute-done.13.pair_b = bf16[2,320,128]{2,1,0:T(8,128)(2,1)S(1)} collective-permute-done((bf16[2,320,128]{2,1,0:T(8,128)(2,1)S(1)}, bf16[2,320,128]{2,1,0:T(8,128)(2,1)S(1)}, u32[]{:S(2)}, u32[]{:S(2)}) %collective-permute-start.13) | collective-permute-done | bytes 163872 | tf_op jit(solution)/shard_map/ppermute | solution.py:313
  87.1 1.5 %closing.1 = f32[1,1,2,320,128]{4,3,2,1,0:T(8,128)} custom-call(bf16[2,320,1920]{2,1,0:T(8,128)(2,1)S(1)} %get-tuple-element.26.merged, bf16[2,320,128]{2,1,0:T(8,128)(2,1)S(1)} %get-tuple-element.24.kept, f32[2,320,128]{2,1,0:T(8,128)S(1)} %get-tuple-element.31.iterate, bf16[2,320,128]{2,1,0:T(8,128)(2,1)S(1)} %get-tuple-element.32.own, ...), custom_call_target="tpu_custom_call" | custom-call | tf_op jit(solution)/shard_map/closing/pallas_call | solution.py:292
Async XLA Ops:
  0.0 38.8 %copy-start = (bf16[1,1,3,320,128]{4,3,2,1,0:T(8,128)(2,1)S(1)}, bf16[1,1,3,320,128]{4,3,2,1,0:T(8,128)(2,1)}, u32[]{:S(2)}) copy-start(bf16[1,1,3,320,128]{4,3,2,1,0:T(8,128)(2,1)} %rhs.3) | copy-start | bytes 737284
  0.0 38.8 %copy-start.3 = (s32[1,1,2]{2,1,0:T(1,128)S(1)}, s32[1,1,2]{2,1,0:T(1,128)}, u32[]{:S(2)}) copy-start(s32[1,1,2]{2,1,0:T(1,128)} %arrival.7) | copy-start | bytes 28
  0.0 49.0 %copy-start.1 = (s32[1,1,2,6]{3,2,1,0:T(2,128)S(1)}, s32[1,1,2,6]{3,2,1,0:T(2,128)}, u32[]{:S(2)}) copy-start(s32[1,1,2,6]{3,2,1,0:T(2,128)} %neighbors.5) | copy-start | bytes 148
  0.0 49.0 %copy-start.2 = (s32[1,1,2,6]{3,2,1,0:T(2,128)S(1)}, s32[1,1,2,6]{3,2,1,0:T(2,128)}, u32[]{:S(2)}) copy-start(s32[1,1,2,6]{3,2,1,0:T(2,128)} %orientation.5) | copy-start | bytes 148
  2.3 42.0 %collective-permute-start.1 = (bf16[320,1664]{1,0:T(8,128)(2,1)S(1)}, bf16[320,1664]{1,0:T(8,128)(2,1)S(1)}, u32[]{:S(2)}, u32[]{:S(2)}) collective-permute-start(bf16[320,1664]{1,0:T(8,128)(2,1)S(1)} %get-tuple-element.20), channel_id=1, source_target_pairs={{0,1},{1,2},{2,3},{3,4},{4,5},{5,6},{6,7},{7,8},{8,9},{9,10},{10,1... | collective-permute-start | bytes 3194888 | tf_op jit(solution)/shard_map/ppermute | solution.py:305
  5.5 46.9 %collective-permute-start.3 = (bf16[320,1664]{1,0:T(8,128)(2,1)S(1)}, bf16[320,1664]{1,0:T(8,128)(2,1)S(1)}, u32[]{:S(2)}, u32[]{:S(2)}) collective-permute-start(bf16[320,1664]{1,0:T(8,128)(2,1)S(1)} %get-tuple-element.20), channel_id=1, source_target_pairs={{1,0},{2,1},{3,2},{4,3},{5,4},{6,5},{7,6},{8,7},{9,8},{10,9},{11,1... | collective-permute-start | bytes 3194888 | tf_op jit(solution)/shard_map/ppermute | solution.py:305
  9.7 26.3 %collective-permute-start = (bf16[320,384]{1,0:T(8,128)(2,1)S(1)}, bf16[320,384]{1,0:T(8,128)(2,1)S(1)}, u32[]{:S(2)}, u32[]{:S(2)}) collective-permute-start(bf16[320,384]{1,0:T(8,128)(2,1)S(1)} %get-tuple-element.19), channel_id=1, source_target_pairs={{0,1},{1,2},{2,3},{3,4},{4,5},{5,6},{6,7},{7,8},{8,9},{9,10},{10,1... | collective-permute-start | bytes 737288 | tf_op jit(solution)/shard_map/ppermute | solution.py:305
  11.7 27.1 %collective-permute-start.2 = (bf16[320,384]{1,0:T(8,128)(2,1)S(1)}, bf16[320,384]{1,0:T(8,128)(2,1)S(1)}, u32[]{:S(2)}, u32[]{:S(2)}) collective-permute-start(bf16[320,384]{1,0:T(8,128)(2,1)S(1)} %get-tuple-element.19), channel_id=1, source_target_pairs={{1,0},{2,1},{3,2},{4,3},{5,4},{6,5},{7,6},{8,7},{9,8},{10,9},{11,1... | collective-permute-start | bytes 737288 | tf_op jit(solution)/shard_map/ppermute | solution.py:305
  17.1 37.1 %collective-permute-start.4 = (bf16[320,320]{1,0:T(8,128)(2,1)S(1)}, bf16[320,320]{1,0:T(8,128)(2,1)S(1)}, u32[]{:S(2)}, u32[]{:S(2)}) collective-permute-start(bf16[320,320]{1,0:T(8,128)(2,1)S(1)} %get-tuple-element.23), channel_id=1, source_target_pairs={{0,1},{1,2},{2,3},{3,4},{4,5},{5,6},{6,7},{7,8},{8,9},{9,10},{10,1... | collective-permute-start | bytes 614408 | tf_op jit(solution)/shard_map/ppermute | solution.py:305
  36.0 18.3 %collective-permute-start.5 = (bf16[320,320]{1,0:T(8,128)(2,1)S(1)}, bf16[320,320]{1,0:T(8,128)(2,1)S(1)}, u32[]{:S(2)}, u32[]{:S(2)}) collective-permute-start(bf16[320,320]{1,0:T(8,128)(2,1)S(1)} %get-tuple-element.23), channel_id=1, source_target_pairs={{1,0},{2,1},{3,2},{4,3},{5,4},{6,5},{7,6},{8,7},{9,8},{10,9},{11,1... | collective-permute-start | bytes 614408 | tf_op jit(solution)/shard_map/ppermute | solution.py:305
  39.4 14.9 %collective-permute-start.6 = (bf16[2,320,128]{2,1,0:T(8,128)(2,1)S(1)}, bf16[2,320,128]{2,1,0:T(8,128)(2,1)S(1)}, u32[]{:S(2)}, u32[]{:S(2)}) collective-permute-start(bf16[2,320,128]{2,1,0:T(8,128)(2,1)S(1)} %get-tuple-element.25.own), channel_id=1, source_target_pairs={{0,16},{16,0},{32,48},{48,32},{64,80},{80,64},{96,112},{112,96},{1... | collective-permute-start | bytes 491528 | tf_op jit(solution)/shard_map/ppermute | solution.py:313
  44.3 10.0 %collective-permute-start.7 = (bf16[2,320,128]{2,1,0:T(8,128)(2,1)S(1)}, bf16[2,320,128]{2,1,0:T(8,128)(2,1)S(1)}, u32[]{:S(2)}, u32[]{:S(2)}) collective-permute-start(bf16[2,320,128]{2,1,0:T(8,128)(2,1)S(1)} %get-tuple-element.25.own), channel_id=1, source_target_pairs={{16,32},{32,16},{48,64},{64,48},{80,96},{96,80},{112,128},{128,112... | collective-permute-start | bytes 491528 | tf_op jit(solution)/shard_map/ppermute | solution.py:313
  56.1 5.7 %collective-permute-start.8 = (bf16[2,320,128]{2,1,0:T(8,128)(2,1)S(1)}, bf16[2,320,128]{2,1,0:T(8,128)(2,1)S(1)}, u32[]{:S(2)}, u32[]{:S(2)}) collective-permute-start(bf16[2,320,128]{2,1,0:T(8,128)(2,1)S(1)} %get-tuple-element.28.own), channel_id=1, source_target_pairs={{0,16},{16,0},{32,48},{48,32},{64,80},{80,64},{96,112},{112,96},{1... | collective-permute-start | bytes 491528 | tf_op jit(solution)/shard_map/ppermute | solution.py:313
  58.0 7.8 %collective-permute-start.9 = (bf16[2,320,128]{2,1,0:T(8,128)(2,1)S(1)}, bf16[2,320,128]{2,1,0:T(8,128)(2,1)S(1)}, u32[]{:S(2)}, u32[]{:S(2)}) collective-permute-start(bf16[2,320,128]{2,1,0:T(8,128)(2,1)S(1)} %get-tuple-element.28.own), channel_id=1, source_target_pairs={{16,32},{32,16},{48,64},{64,48},{80,96},{96,80},{112,128},{128,112... | collective-permute-start | bytes 491528 | tf_op jit(solution)/shard_map/ppermute | solution.py:313
  66.7 5.7 %collective-permute-start.10 = (bf16[2,320,128]{2,1,0:T(8,128)(2,1)S(1)}, bf16[2,320,128]{2,1,0:T(8,128)(2,1)S(1)}, u32[]{:S(2)}, u32[]{:S(2)}) collective-permute-start(bf16[2,320,128]{2,1,0:T(8,128)(2,1)S(1)} %get-tuple-element.30.own), channel_id=1, source_target_pairs={{0,16},{16,0},{32,48},{48,32},{64,80},{80,64},{96,112},{112,96},{1... | collective-permute-start | bytes 491528 | tf_op jit(solution)/shard_map/ppermute | solution.py:313
  68.6 7.8 %collective-permute-start.11 = (bf16[2,320,128]{2,1,0:T(8,128)(2,1)S(1)}, bf16[2,320,128]{2,1,0:T(8,128)(2,1)S(1)}, u32[]{:S(2)}, u32[]{:S(2)}) collective-permute-start(bf16[2,320,128]{2,1,0:T(8,128)(2,1)S(1)} %get-tuple-element.30.own), channel_id=1, source_target_pairs={{16,32},{32,16},{48,64},{64,48},{80,96},{96,80},{112,128},{128,112... | collective-permute-start | bytes 491528 | tf_op jit(solution)/shard_map/ppermute | solution.py:313
  77.3 5.7 %collective-permute-start.12 = (bf16[2,320,128]{2,1,0:T(8,128)(2,1)S(1)}, bf16[2,320,128]{2,1,0:T(8,128)(2,1)S(1)}, u32[]{:S(2)}, u32[]{:S(2)}) collective-permute-start(bf16[2,320,128]{2,1,0:T(8,128)(2,1)S(1)} %get-tuple-element.32.own), channel_id=1, source_target_pairs={{0,16},{16,0},{32,48},{48,32},{64,80},{80,64},{96,112},{112,96},{1... | collective-permute-start | bytes 491528 | tf_op jit(solution)/shard_map/ppermute | solution.py:313
  79.2 7.8 %collective-permute-start.13 = (bf16[2,320,128]{2,1,0:T(8,128)(2,1)S(1)}, bf16[2,320,128]{2,1,0:T(8,128)(2,1)S(1)}, u32[]{:S(2)}, u32[]{:S(2)}) collective-permute-start(bf16[2,320,128]{2,1,0:T(8,128)(2,1)S(1)} %get-tuple-element.32.own), channel_id=1, source_target_pairs={{16,32},{32,16},{48,64},{64,48},{80,96},{96,80},{112,128},{128,112... | collective-permute-start | bytes 491528 | tf_op jit(solution)/shard_map/ppermute | solution.py:313

commit v3 on v2

--- a/solution.py
+++ b/solution.py
@@ -41,11 +41,12 @@
 ANY_SPEC = pl.BlockSpec(memory_space=pl.ANY)
 
 
-def turned_select(start, n, k, parity):
+def turned_select(start, n, k):
     shift = start % TILE
     layer = n // 2
-    first = jnp.where(parity == 0, layer == 2, layer == 0)
-    slot = jnp.where(layer == 1, 1, jnp.where(first, 2, 4) + n % 2)
+    here = lax.axis_index("gx")
+    outside = ((layer == 0) & (here == 0)) | ((layer == 2) & (here == lax.axis_size("gx") - 1))
+    slot = jnp.where(layer == 1, 1, jnp.where(layer == 0, 2, 4) + n % 2)
     place = DOF * slot
     tile = place // TILE
     column = lax.broadcasted_iota(jnp.int32, (1, SPAN * TILE), 1) - (place - tile * TILE)
@@ -54,15 +55,15 @@
     source_a = jnp.where(k == 0, a, jnp.where(k == 1, 3 - b, jnp.where(k == 2, 3 - a, b)))
     source_b = jnp.where(k == 0, b, jnp.where(k == 1, a, jnp.where(k == 2, 3 - b, 3 - a)))
     source = shift + (column // 64) * 64 + source_a * 16 + source_b * 4 + column % 4
-    source = jnp.where((column >= 0) & (column < DOF), source, -1)
+    source = jnp.where((column >= 0) & (column < DOF) & jnp.logical_not(outside), source, -1)
     rows = lax.broadcasted_iota(jnp.int32, (DOF + shift, SPAN * TILE), 0)
     return tile, jnp.where(rows == source, 1.0, 0.0).astype(jnp.bfloat16)
 
 
-def add_faces(faces, columns, neighbor, turn, parity, acc_ref):
+def add_faces(faces, columns, neighbor, turn, acc_ref):
     for face in faces:
         start = DOF * (face + 1)
-        tile, select = turned_select(start, neighbor(face), turn(face), parity)
+        tile, select = turned_select(start, neighbor(face), turn(face))
         base = start - start % TILE
         moved = jnp.dot(columns(base, start + DOF), select, preferred_element_type=jnp.float32)
         for part in range(SPAN):
@@ -140,7 +141,6 @@
 
 
 def local_kernel(arrival, neighbors, orientation, blocks, merged, rows, acc, sems):
-    parity = lax.axis_index("gx") % 2
     copies = [
         pltpu.make_async_copy(blocks.at[0, 0, jnp.clip(arrival[0, 0, q], 0, 2)], rows.at[q], sems.at[q])
         for q in range(KEPT)
@@ -156,7 +156,7 @@
             put_own(columns, acc)
             neighbor = lambda face: neighbors[0, 0, q, face]
             turn = lambda face: orientation[0, 0, q, face]
-            add_faces(range(FACES), columns, neighbor, turn, parity, acc)
+            add_faces(range(FACES), columns, neighbor, turn, acc)
             for tile in range(TILES):
                 merged[q, :, tile * TILE : (tile + 1) * TILE] = acc[tile].astype(jnp.bfloat16)
 
@@ -181,7 +181,6 @@
     arrival, neighbors, orientation, local, lo_head, lo_middle, hi_head, hi_middle, merged, acc
 ):
     del local
-    parity = lax.axis_index("gx") % 2
     for q in range(KEPT):
         for code, head, middle in ((3, lo_head, lo_middle), (4, hi_head, hi_middle)):
 
@@ -195,7 +194,7 @@
                 put_own(columns, acc.at[q])
                 neighbor = lambda face: neighbors[0, 0, q, face]
                 turn = lambda face: orientation[0, 0, q, face]
-                add_faces(range(FACES - 1), columns, neighbor, turn, parity, acc.at[q])
+                add_faces(range(FACES - 1), columns, neighbor, turn, acc.at[q])
                 for tile in range(TILES):
                     merged[q, :, tile * TILE : (tile + 1) * TILE] = acc[q, tile].astype(jnp.bfloat16)
 
@@ -215,8 +214,8 @@
     )(arrival, neighbors, orientation, *near(local, lo_head, lo_middle, hi_head, hi_middle))
 
 
-def applied_rows(merged, own, pair_a, pair_b):
-    far = jnp.concatenate([pair_a[0], pair_a[1], pair_b[0], pair_b[1]], axis=0)
+def applied_rows(merged, own, below, above):
+    far = jnp.concatenate([below[0], below[1], above[0], above[1]], axis=0)
     for q in range(KEPT):
         near = jnp.concatenate([own[q], own[1 - q]], axis=0)
         applied = jnp.dot(merged[q, :, 0 : 2 * DOF], near, preferred_element_type=jnp.float32)
@@ -225,31 +224,30 @@
 
 
 def opening_kernel(
-    arrival, neighbors, orientation, partial, acc, lo_last, hi_last, kept, own, pair_a, pair_b, merged, iterate, rounded
+    arrival, neighbors, orientation, partial, acc, lo_last, hi_last, kept, own, below, above, merged, iterate, rounded
 ):
     del partial
-    parity = lax.axis_index("gx") % 2
     for q in range(KEPT):
         for code, last in ((3, lo_last), (4, hi_last)):
 
             @pl.when(arrival[0, 0, q] == code)
             def _():
                 face = FACES - 1
-                tile, select = turned_select(LAST, neighbors[0, 0, q, face], orientation[0, 0, q, face], parity)
+                tile, select = turned_select(LAST, neighbors[0, 0, q, face], orientation[0, 0, q, face])
                 moved = jnp.dot(last[...], select, preferred_element_type=jnp.float32)
                 for part in range(SPAN):
                     total = acc[q, tile + part] + moved[:, part * TILE : (part + 1) * TILE]
                     place = pl.multiple_of((tile + part) * TILE, TILE)
                     merged[q, :, pl.ds(place, TILE)] = total.astype(jnp.bfloat16)
 
-    for q, applied in applied_rows(merged, own, pair_a, pair_b):
+    for q, applied in applied_rows(merged, own, below, above):
         side = kept[q].astype(jnp.float32)
         value = RELAXATION * side + RELAXATION * (side - applied)
         iterate[q] = value
         rounded[q] = value.astype(jnp.bfloat16)
 
 
-def opening(arrival, neighbors, orientation, partial, acc, lo_last, hi_last, kept, own, pair_a, pair_b):
+def opening(arrival, neighbors, orientation, partial, acc, lo_last, hi_last, kept, own, below, above):
     return pl.pallas_call(
         opening_kernel,
         in_specs=[SMEM_SPEC] * 3 + [VMEM_SPEC] * 8,
@@ -262,17 +260,17 @@
         input_output_aliases={3: 0},
         compiler_params=PARAMS,
         name="opening",
-    )(arrival, neighbors, orientation, *near(partial, acc, lo_last, hi_last, kept, own, pair_a, pair_b))
-
-
-def middle_kernel(merged, kept, iterate, own, pair_a, pair_b, iterate_out, rounded):
-    for q, applied in applied_rows(merged, own, pair_a, pair_b):
+    )(arrival, neighbors, orientation, *near(partial, acc, lo_last, hi_last, kept, own, below, above))
+
+
+def middle_kernel(merged, kept, iterate, own, below, above, iterate_out, rounded):
+    for q, applied in applied_rows(merged, own, below, above):
         value = iterate[q] + RELAXATION * (kept[q].astype(jnp.float32) - applied)
         iterate_out[q] = value
         rounded[q] = value.astype(jnp.bfloat16)
 
 
-def middle(merged, kept, iterate, own, pair_a, pair_b):
+def middle(merged, kept, iterate, own, below, above):
     return pl.pallas_call(
         middle_kernel,
         in_specs=[VMEM_SPEC] * 6,
@@ -280,15 +278,15 @@
         out_shape=[vmem((KEPT, DOF, RHS), jnp.float32), vmem((KEPT, DOF, RHS), jnp.bfloat16)],
         compiler_params=PARAMS,
         name="middle",
-    )(*near(merged, kept, iterate, own, pair_a, pair_b))
-
-
-def closing_kernel(merged, kept, iterate, own, pair_a, pair_b, smoothed):
-    for q, applied in applied_rows(merged, own, pair_a, pair_b):
+    )(*near(merged, kept, iterate, own, below, above))
+
+
+def closing_kernel(merged, kept, iterate, own, below, above, smoothed):
+    for q, applied in applied_rows(merged, own, below, above):
         smoothed[0, 0, q] = iterate[q] + RELAXATION * (kept[q].astype(jnp.float32) - applied)
 
 
-def closing(merged, kept, iterate, own, pair_a, pair_b):
+def closing(merged, kept, iterate, own, below, above):
     return pl.pallas_call(
         closing_kernel,
         in_specs=[VMEM_SPEC] * 6,
@@ -296,32 +294,26 @@
         out_shape=jax.ShapeDtypeStruct((1, 1, KEPT, DOF, RHS), jnp.float32),
         compiler_params=PARAMS,
         name="closing",
-    )(*near(merged, kept, iterate, own, pair_a, pair_b))
-
-
-def shifted(value, axis, steps):
+    )(*near(merged, kept, iterate, own, below, above))
+
+
+def shifted(value, axis, steps, closed):
     count = lax.axis_size(axis)
-    leading, last = (max(0, -steps), min(count, count - steps))
-    return lax.ppermute(value, axis, [(source, source + steps) for source in range(leading, last)])
-
-
-def swapped(value, axis, start):
-    count = lax.axis_size(axis)
-    pairs = []
-    for low in range(start, count - 1, 2):
-        pairs += [(low, low + 1), (low + 1, low)]
+    pairs = [(source, (source + steps) % count) for source in range(count)]
+    if not closed:
+        pairs = [(source, target) for source, target in pairs if target == source + steps]
     return lax.ppermute(value, axis, pairs)
 
 
 def halo(rounded):
-    pair_b = swapped(rounded, "gx", 1)
-    pair_a = swapped(rounded, "gx", 0)
-    return pair_a, pair_b
+    below = shifted(rounded, "gx", 1, closed=True)
+    above = shifted(rounded, "gx", -1, closed=True)
+    return below, above
 
 
 def both_ways(value):
-    lower = shifted(value, "gy", 1)
-    upper = shifted(value, "gy", -1)
+    lower = shifted(value, "gy", 1, closed=False)
+    upper = shifted(value, "gy", -1, closed=False)
     return lower, upper
 
 
@@ -331,19 +323,19 @@
     lo_middle, hi_middle = both_ways(middle_columns)
     lo_last, hi_last = both_ways(last)
     kept, own = first(arrival, right_side, lo_head, hi_head)
-    pair_a, pair_b = halo(own)
+    below, above = halo(own)
     local = merged_local(arrival, neighbors, orientation, blocks)
     partial, acc = merged_arrived(
         arrival, neighbors, orientation, local, lo_head, lo_middle, hi_head, hi_middle
     )
     merged, iterate, own = opening(
-        arrival, neighbors, orientation, partial, acc, lo_last, hi_last, kept, own, pair_a, pair_b
+        arrival, neighbors, orientation, partial, acc, lo_last, hi_last, kept, own, below, above
     )
     for _ in range(1, ITERS - 1):
-        pair_a, pair_b = halo(own)
-        iterate, own = middle(merged, kept, iterate, own, pair_a, pair_b)
-    pair_a, pair_b = halo(own)
-    return closing(merged, kept, iterate, own, pair_a, pair_b)
+        below, above = halo(own)
+        iterate, own = middle(merged, kept, iterate, own, below, above)
+    below, above = halo(own)
+    return closing(merged, kept, iterate, own, below, above)
 
 
 def solution(mesh):

time: 89.1 us -> 77.1 us (0.87)
  the two profiles are of different devices: /device:TPU:103 before, /device:TPU:6 now
where the time goes in v3:
time: 77.1 us; the launch traced here: 76.8 us
  starting transfers between devices  36.5 us (47%)
  waiting for transfers between devices  26.8 us (35%)
  Pallas kernels  13.3 us (17%)
    ppermute x14, starting transfers between devices, shifted(): return lax.ppermute(value, axis, pairs)  36.5 us
    ppermute x14, waiting for transfers between devices, shifted(): return lax.ppermute(value, axis, pairs)  26.8 us
    pallas_call x1, Pallas kernels, merged_local(): pl.pallas_call(local_kernel, in_specs=[SMEM_SPEC] * 3 + [ANY_SPEC], out_s...  3.41 us
    pallas_call x1, Pallas kernels, pick(): pl.pallas_call(pick_kernel, in_specs=[SMEM_SPEC] + [ANY_SPEC] * 2, out_sp...  2.3 us
    pallas_call x1, Pallas kernels, opening(): pl.pallas_call(opening_kernel, in_specs=[SMEM_SPEC] * 3 + [VMEM_SPEC] * 8...  1.96 us
    pallas_call x1, Pallas kernels, merged_arrived(): pl.pallas_call(arrived_kernel, in_specs=[SMEM_SPEC] * 3 + [VMEM_SPEC] * 5...  1.91 us
    pallas_call x2, Pallas kernels, middle(): pl.pallas_call(middle_kernel, in_specs=[VMEM_SPEC] * 6, out_specs=[VMEM_S...  1.59 us
  transfers between devices with their start and end apart: 14, of which 4 were waited for; matrix products, arithmetic and copies ran while one was open for 0% of the time, Pallas kernels for 8%

profile of v3, /device:TPU:6, one launch (start us, length us, event | category | flops | bytes accessed | tf_op | source)
XLA Modules:
  0.0 76.8 jit_solution(2668237364493940740)
XLA Ops:
  0.0 0.0 copy-start
  0.0 0.0 copy-start.3
  0.0 0.0 copy-start.1
  0.0 0.0 copy-start.2
  0.0 2.3 %pick.1 = (bf16[320,384]{1,0:T(8,128)(2,1)S(1)}, bf16[320,1664]{1,0:T(8,128)(2,1)S(1)}, bf16[320,320]{1,0:T(8,128)(2,1)S(1)}) custom-call(s32[1,1,2]{2,1,0:T(1,128)} %departure.1, bf16[1,1,3,320,2240]{4,3,2,1,0:T(8,128)(2,1)} %blocks.3, bf16[1,1,3,320,128]{4,3,2,1,0:T(8,128)(2,1)} %rhs.3), custom_call_target="tpu_custom_call" | custom-call | tf_op jit(solution)/shard_map/pick/pallas_call | solution.py:97
  2.3 3.5 %collective-permute-start.1 = (bf16[320,1664]{1,0:T(8,128)(2,1)S(1)}, bf16[320,1664]{1,0:T(8,128)(2,1)S(1)}, u32[]{:S(2)}, u32[]{:S(2)}) collective-permute-start(bf16[320,1664]{1,0:T(8,128)(2,1)S(1)} %get-tuple-element.20), channel_id=1, source_target_pairs={{0,1},{1,2},{2,3},{3,4},{4,5},{5,6},{6,7},{7,8},{8,9},{9,10},{10,1... | collective-permute-start | bytes 3194888 | tf_op jit(solution)/shard_map/ppermute | solution.py:305
  5.8 4.5 %collective-permute-start.3 = (bf16[320,1664]{1,0:T(8,128)(2,1)S(1)}, bf16[320,1664]{1,0:T(8,128)(2,1)S(1)}, u32[]{:S(2)}, u32[]{:S(2)}) collective-permute-start(bf16[320,1664]{1,0:T(8,128)(2,1)S(1)} %get-tuple-element.20), channel_id=1, source_target_pairs={{1,0},{2,1},{3,2},{4,3},{5,4},{6,5},{7,6},{8,7},{9,8},{10,9},{11,1... | collective-permute-start | bytes 3194888 | tf_op jit(solution)/shard_map/ppermute | solution.py:305
  10.3 1.9 %collective-permute-start = (bf16[320,384]{1,0:T(8,128)(2,1)S(1)}, bf16[320,384]{1,0:T(8,128)(2,1)S(1)}, u32[]{:S(2)}, u32[]{:S(2)}) collective-permute-start(bf16[320,384]{1,0:T(8,128)(2,1)S(1)} %get-tuple-element.19), channel_id=1, source_target_pairs={{0,1},{1,2},{2,3},{3,4},{4,5},{5,6},{6,7},{7,8},{8,9},{9,10},{10,1... | collective-permute-start | bytes 737288 | tf_op jit(solution)/shard_map/ppermute | solution.py:305
  12.2 6.0 %collective-permute-start.2 = (bf16[320,384]{1,0:T(8,128)(2,1)S(1)}, bf16[320,384]{1,0:T(8,128)(2,1)S(1)}, u32[]{:S(2)}, u32[]{:S(2)}) collective-permute-start(bf16[320,384]{1,0:T(8,128)(2,1)S(1)} %get-tuple-element.19), channel_id=1, source_target_pairs={{1,0},{2,1},{3,2},{4,3},{5,4},{6,5},{7,6},{8,7},{9,8},{10,9},{11,1... | collective-permute-start | bytes 737288 | tf_op jit(solution)/shard_map/ppermute | solution.py:305
  18.3 1.9 %collective-permute-start.4 = (bf16[320,320]{1,0:T(8,128)(2,1)S(1)}, bf16[320,320]{1,0:T(8,128)(2,1)S(1)}, u32[]{:S(2)}, u32[]{:S(2)}) collective-permute-start(bf16[320,320]{1,0:T(8,128)(2,1)S(1)} %get-tuple-element.23), channel_id=1, source_target_pairs={{0,1},{1,2},{2,3},{3,4},{4,5},{5,6},{6,7},{7,8},{8,9},{9,10},{10,1... | collective-permute-start | bytes 614408 | tf_op jit(solution)/shard_map/ppermute | solution.py:305
  20.2 17.8 %collective-permute-done.lo_head.lower = bf16[320,384]{1,0:T(8,128)(2,1)S(1)} collective-permute-done((bf16[320,384]{1,0:T(8,128)(2,1)S(1)}, bf16[320,384]{1,0:T(8,128)(2,1)S(1)}, u32[]{:S(2)}, u32[]{:S(2)}) %collective-permute-start) | collective-permute-done | bytes 245792 | tf_op jit(solution)/shard_map/ppermute | solution.py:305
  38.0 3.1 %collective-permute-start.5 = (bf16[320,320]{1,0:T(8,128)(2,1)S(1)}, bf16[320,320]{1,0:T(8,128)(2,1)S(1)}, u32[]{:S(2)}, u32[]{:S(2)}) collective-permute-start(bf16[320,320]{1,0:T(8,128)(2,1)S(1)} %get-tuple-element.23), channel_id=1, source_target_pairs={{1,0},{2,1},{3,2},{4,3},{5,4},{6,5},{7,6},{8,7},{9,8},{10,9},{11,1... | collective-permute-start | bytes 614408 | tf_op jit(solution)/shard_map/ppermute | solution.py:305
  41.1 0.0 collective-permute-done.2.hi_head.upper
  41.1 0.0 copy-done
  41.1 0.0 copy-done.3
  41.1 0.6 first.1
  41.7 0.0 collective-permute-start.6
  41.7 0.0 collective-permute-done.1.lo_middle
  41.7 6.7 %collective-permute-start.7 = (bf16[2,320,128]{2,1,0:T(8,128)(2,1)S(1)}, bf16[2,320,128]{2,1,0:T(8,128)(2,1)S(1)}, u32[]{:S(2)}, u32[]{:S(2)}) collective-permute-start(bf16[2,320,128]{2,1,0:T(8,128)(2,1)S(1)} %get-tuple-element.25.own), channel_id=1, source_target_pairs={{0,496},{16,0},{32,16},{48,32},{64,48},{80,64},{96,80},{112,96},{1... | collective-permute-start | bytes 491528 | tf_op jit(solution)/shard_map/ppermute | solution.py:305
  48.4 0.0 copy-done.1
  48.4 0.0 copy-done.2
  48.4 3.4 %merge_local.1.local = bf16[2,320,1920]{2,1,0:T(8,128)(2,1)S(1)} custom-call(s32[1,1,2]{2,1,0:T(1,128)S(1)} %copy-done.3, s32[1,1,2,6]{3,2,1,0:T(2,128)S(1)} %copy-done.1, s32[1,1,2,6]{3,2,1,0:T(2,128)S(1)} %copy-done.2, bf16[1,1,3,320,2240]{4,3,2,1,0:T(8,128)(2,1)} %blocks.3), custom_call_target="tpu_custom_call" | custom-call | tf_op jit(solution)/shard_map/merge_local/pallas_call | solution.py:165
  51.8 0.0 collective-permute-done.3.hi_middle
  51.9 1.9 %merge_arrived.1 = (bf16[2,320,1920]{2,1,0:T(8,128)(2,1)S(1)}, f32[2,15,320,128]{3,2,1,0:T(8,128)S(1)}) custom-call(s32[1,1,2]{2,1,0:T(1,128)S(1)} %copy-done.3, s32[1,1,2,6]{3,2,1,0:T(2,128)S(1)} %copy-done.1, s32[1,1,2,6]{3,2,1,0:T(2,128)S(1)} %copy-done.2, bf16[2,320,1920]{2,1,0:T(8,128)(2,1)S(1)} %merge_local.1.local, ...), custom_call_target="tpu_custom_call", output_to_operand_aliasing={{0}: (3, {})} | custom-call | tf_op jit(solution)/shard_map/merge_arrived/pallas_call | solution.py:203
  53.8 0.0 collective-permute-done.4.lo_last
  53.8 0.0 collective-permute-done.5.hi_last
  53.8 0.0 collective-permute-done.6.below
  53.8 0.0 collective-permute-done.7.above
  53.8 2.0 %opening.1 = (bf16[2,320,1920]{2,1,0:T(8,128)(2,1)S(1)}, f32[2,320,128]{2,1,0:T(8,128)S(1)}, bf16[2,320,128]{2,1,0:T(8,128)(2,1)S(1)}) custom-call(s32[1,1,2]{2,1,0:T(1,128)S(1)} %copy-done.3, s32[1,1,2,6]{3,2,1,0:T(2,128)S(1)} %copy-done.1, s32[1,1,2,6]{3,2,1,0:T(2,128)S(1)} %copy-done.2, ...), custom_call_target="tpu_custom_call", output_to_operand_aliasing={{0}: (3, {})} | custom-call | tf_op jit(solution)/shard_map/opening/pallas_call | solution.py:251
  55.8 0.0 collective-permute-start.8
  55.8 2.9 %collective-permute-start.9 = (bf16[2,320,128]{2,1,0:T(8,128)(2,1)S(1)}, bf16[2,320,128]{2,1,0:T(8,128)(2,1)S(1)}, u32[]{:S(2)}, u32[]{:S(2)}) collective-permute-start(bf16[2,320,128]{2,1,0:T(8,128)(2,1)S(1)} %get-tuple-element.28.own), channel_id=1, source_target_pairs={{0,496},{16,0},{32,16},{48,32},{64,48},{80,64},{96,80},{112,96},{1... | collective-permute-start | bytes 491528 | tf_op jit(solution)/shard_map/ppermute | solution.py:305
  58.7 3.0 %collective-permute-done.8.below = bf16[2,320,128]{2,1,0:T(8,128)(2,1)S(1)} collective-permute-done((bf16[2,320,128]{2,1,0:T(8,128)(2,1)S(1)}, bf16[2,320,128]{2,1,0:T(8,128)(2,1)S(1)}, u32[]{:S(2)}, u32[]{:S(2)}) %collective-permute-start.8) | collective-permute-done | bytes 163872 | tf_op jit(solution)/shard_map/ppermute | solution.py:305
  61.7 0.0 collective-permute-done.9.above
  61.7 0.8 %middle.2 = (f32[2,320,128]{2,1,0:T(8,128)S(1)}, bf16[2,320,128]{2,1,0:T(8,128)(2,1)S(1)}) custom-call(bf16[2,320,1920]{2,1,0:T(8,128)(2,1)S(1)} %get-tuple-element.26.merged, bf16[2,320,128]{2,1,0:T(8,128)(2,1)S(1)} %get-tuple-element.24.kept, f32[2,320,128]{2,1,0:T(8,128)S(1)} %get-tuple-element.27.iterate, ...), custom_call_target="tpu_custom_call" | custom-call | tf_op jit(solution)/shard_map/middle/pallas_call | solution.py:274
  62.5 0.0 collective-permute-start.10
  62.6 3.0 %collective-permute-start.11 = (bf16[2,320,128]{2,1,0:T(8,128)(2,1)S(1)}, bf16[2,320,128]{2,1,0:T(8,128)(2,1)S(1)}, u32[]{:S(2)}, u32[]{:S(2)}) collective-permute-start(bf16[2,320,128]{2,1,0:T(8,128)(2,1)S(1)} %get-tuple-element.30.own), channel_id=1, source_target_pairs={{0,496},{16,0},{32,16},{48,32},{64,48},{80,64},{96,80},{112,96},{1... | collective-permute-start | bytes 491528 | tf_op jit(solution)/shard_map/ppermute | solution.py:305
  65.5 3.0 %collective-permute-done.10.below = bf16[2,320,128]{2,1,0:T(8,128)(2,1)S(1)} collective-permute-done((bf16[2,320,128]{2,1,0:T(8,128)(2,1)S(1)}, bf16[2,320,128]{2,1,0:T(8,128)(2,1)S(1)}, u32[]{:S(2)}, u32[]{:S(2)}) %collective-permute-start.10) | collective-permute-done | bytes 163872 | tf_op jit(solution)/shard_map/ppermute | solution.py:305
  68.5 0.0 collective-permute-done.11.above
  68.5 0.8 %middle.3 = (f32[2,320,128]{2,1,0:T(8,128)S(1)}, bf16[2,320,128]{2,1,0:T(8,128)(2,1)S(1)}) custom-call(bf16[2,320,1920]{2,1,0:T(8,128)(2,1)S(1)} %get-tuple-element.26.merged, bf16[2,320,128]{2,1,0:T(8,128)(2,1)S(1)} %get-tuple-element.24.kept, f32[2,320,128]{2,1,0:T(8,128)S(1)} %get-tuple-element.29.iterate, ...), custom_call_target="tpu_custom_call" | custom-call | tf_op jit(solution)/shard_map/middle/pallas_call | solution.py:274
  69.3 0.0 collective-permute-start.12
  69.4 3.0 %collective-permute-start.13 = (bf16[2,320,128]{2,1,0:T(8,128)(2,1)S(1)}, bf16[2,320,128]{2,1,0:T(8,128)(2,1)S(1)}, u32[]{:S(2)}, u32[]{:S(2)}) collective-permute-start(bf16[2,320,128]{2,1,0:T(8,128)(2,1)S(1)} %get-tuple-element.32.own), channel_id=1, source_target_pairs={{0,496},{16,0},{32,16},{48,32},{64,48},{80,64},{96,80},{112,96},{1... | collective-permute-start | bytes 491528 | tf_op jit(solution)/shard_map/ppermute | solution.py:305
  72.3 3.0 %collective-permute-done.12.below = bf16[2,320,128]{2,1,0:T(8,128)(2,1)S(1)} collective-permute-done((bf16[2,320,128]{2,1,0:T(8,128)(2,1)S(1)}, bf16[2,320,128]{2,1,0:T(8,128)(2,1)S(1)}, u32[]{:S(2)}, u32[]{:S(2)}) %collective-permute-start.12) | collective-permute-done | bytes 163872 | tf_op jit(solution)/shard_map/ppermute | solution.py:305
  75.3 0.0 collective-permute-done.13.above
  75.3 1.5 %closing.1 = f32[1,1,2,320,128]{4,3,2,1,0:T(8,128)} custom-call(bf16[2,320,1920]{2,1,0:T(8,128)(2,1)S(1)} %get-tuple-element.26.merged, bf16[2,320,128]{2,1,0:T(8,128)(2,1)S(1)} %get-tuple-element.24.kept, f32[2,320,128]{2,1,0:T(8,128)S(1)} %get-tuple-element.31.iterate, bf16[2,320,128]{2,1,0:T(8,128)(2,1)S(1)} %get-tuple-element.32.own, ...), custom_call_target="tpu_custom_call" | custom-call | tf_op jit(solution)/shard_map/closing/pallas_call | solution.py:290
Async XLA Ops:
  0.0 41.1 %copy-start = (bf16[1,1,3,320,128]{4,3,2,1,0:T(8,128)(2,1)S(1)}, bf16[1,1,3,320,128]{4,3,2,1,0:T(8,128)(2,1)}, u32[]{:S(2)}) copy-start(bf16[1,1,3,320,128]{4,3,2,1,0:T(8,128)(2,1)} %rhs.3) | copy-start | bytes 737284
  0.0 41.1 %copy-start.3 = (s32[1,1,2]{2,1,0:T(1,128)S(1)}, s32[1,1,2]{2,1,0:T(1,128)}, u32[]{:S(2)}) copy-start(s32[1,1,2]{2,1,0:T(1,128)} %arrival.7) | copy-start | bytes 28
  0.0 48.4 %copy-start.1 = (s32[1,1,2,6]{3,2,1,0:T(2,128)S(1)}, s32[1,1,2,6]{3,2,1,0:T(2,128)}, u32[]{:S(2)}) copy-start(s32[1,1,2,6]{3,2,1,0:T(2,128)} %neighbors.5) | copy-start | bytes 148
  0.0 48.4 %copy-start.2 = (s32[1,1,2,6]{3,2,1,0:T(2,128)S(1)}, s32[1,1,2,6]{3,2,1,0:T(2,128)}, u32[]{:S(2)}) copy-start(s32[1,1,2,6]{3,2,1,0:T(2,128)} %orientation.5) | copy-start | bytes 148
  2.3 39.4 %collective-permute-start.1 = (bf16[320,1664]{1,0:T(8,128)(2,1)S(1)}, bf16[320,1664]{1,0:T(8,128)(2,1)S(1)}, u32[]{:S(2)}, u32[]{:S(2)}) collective-permute-start(bf16[320,1664]{1,0:T(8,128)(2,1)S(1)} %get-tuple-element.20), channel_id=1, source_target_pairs={{0,1},{1,2},{2,3},{3,4},{4,5},{5,6},{6,7},{7,8},{8,9},{9,10},{10,1... | collective-permute-start | bytes 3194888 | tf_op jit(solution)/shard_map/ppermute | solution.py:305
  5.8 46.0 %collective-permute-start.3 = (bf16[320,1664]{1,0:T(8,128)(2,1)S(1)}, bf16[320,1664]{1,0:T(8,128)(2,1)S(1)}, u32[]{:S(2)}, u32[]{:S(2)}) collective-permute-start(bf16[320,1664]{1,0:T(8,128)(2,1)S(1)} %get-tuple-element.20), channel_id=1, source_target_pairs={{1,0},{2,1},{3,2},{4,3},{5,4},{6,5},{7,6},{8,7},{9,8},{10,9},{11,1... | collective-permute-start | bytes 3194888 | tf_op jit(solution)/shard_map/ppermute | solution.py:305
  10.3 27.7 %collective-permute-start = (bf16[320,384]{1,0:T(8,128)(2,1)S(1)}, bf16[320,384]{1,0:T(8,128)(2,1)S(1)}, u32[]{:S(2)}, u32[]{:S(2)}) collective-permute-start(bf16[320,384]{1,0:T(8,128)(2,1)S(1)} %get-tuple-element.19), channel_id=1, source_target_pairs={{0,1},{1,2},{2,3},{3,4},{4,5},{5,6},{6,7},{7,8},{8,9},{9,10},{10,1... | collective-permute-start | bytes 737288 | tf_op jit(solution)/shard_map/ppermute | solution.py:305
  12.2 28.8 %collective-permute-start.2 = (bf16[320,384]{1,0:T(8,128)(2,1)S(1)}, bf16[320,384]{1,0:T(8,128)(2,1)S(1)}, u32[]{:S(2)}, u32[]{:S(2)}) collective-permute-start(bf16[320,384]{1,0:T(8,128)(2,1)S(1)} %get-tuple-element.19), channel_id=1, source_target_pairs={{1,0},{2,1},{3,2},{4,3},{5,4},{6,5},{7,6},{8,7},{9,8},{10,9},{11,1... | collective-permute-start | bytes 737288 | tf_op jit(solution)/shard_map/ppermute | solution.py:305
  18.3 35.5 %collective-permute-start.4 = (bf16[320,320]{1,0:T(8,128)(2,1)S(1)}, bf16[320,320]{1,0:T(8,128)(2,1)S(1)}, u32[]{:S(2)}, u32[]{:S(2)}) collective-permute-start(bf16[320,320]{1,0:T(8,128)(2,1)S(1)} %get-tuple-element.23), channel_id=1, source_target_pairs={{0,1},{1,2},{2,3},{3,4},{4,5},{5,6},{6,7},{7,8},{8,9},{9,10},{10,1... | collective-permute-start | bytes 614408 | tf_op jit(solution)/shard_map/ppermute | solution.py:305
  38.0 15.8 %collective-permute-start.5 = (bf16[320,320]{1,0:T(8,128)(2,1)S(1)}, bf16[320,320]{1,0:T(8,128)(2,1)S(1)}, u32[]{:S(2)}, u32[]{:S(2)}) collective-permute-start(bf16[320,320]{1,0:T(8,128)(2,1)S(1)} %get-tuple-element.23), channel_id=1, source_target_pairs={{1,0},{2,1},{3,2},{4,3},{5,4},{6,5},{7,6},{8,7},{9,8},{10,9},{11,1... | collective-permute-start | bytes 614408 | tf_op jit(solution)/shard_map/ppermute | solution.py:305
  41.7 12.1 %collective-permute-start.6 = (bf16[2,320,128]{2,1,0:T(8,128)(2,1)S(1)}, bf16[2,320,128]{2,1,0:T(8,128)(2,1)S(1)}, u32[]{:S(2)}, u32[]{:S(2)}) collective-permute-start(bf16[2,320,128]{2,1,0:T(8,128)(2,1)S(1)} %get-tuple-element.25.own), channel_id=1, source_target_pairs={{0,16},{16,32},{32,48},{48,64},{64,80},{80,96},{96,112},{112,128},... | collective-permute-start | bytes 491528 | tf_op jit(solution)/shard_map/ppermute | solution.py:305
  41.7 12.1 %collective-permute-start.7 = (bf16[2,320,128]{2,1,0:T(8,128)(2,1)S(1)}, bf16[2,320,128]{2,1,0:T(8,128)(2,1)S(1)}, u32[]{:S(2)}, u32[]{:S(2)}) collective-permute-start(bf16[2,320,128]{2,1,0:T(8,128)(2,1)S(1)} %get-tuple-element.25.own), channel_id=1, source_target_pairs={{0,496},{16,0},{32,16},{48,32},{64,48},{80,64},{96,80},{112,96},{1... | collective-permute-start | bytes 491528 | tf_op jit(solution)/shard_map/ppermute | solution.py:305
  55.8 6.0 %collective-permute-start.8 = (bf16[2,320,128]{2,1,0:T(8,128)(2,1)S(1)}, bf16[2,320,128]{2,1,0:T(8,128)(2,1)S(1)}, u32[]{:S(2)}, u32[]{:S(2)}) collective-permute-start(bf16[2,320,128]{2,1,0:T(8,128)(2,1)S(1)} %get-tuple-element.28.own), channel_id=1, source_target_pairs={{0,16},{16,32},{32,48},{48,64},{64,80},{80,96},{96,112},{112,128},... | collective-permute-start | bytes 491528 | tf_op jit(solution)/shard_map/ppermute | solution.py:305
  55.8 5.9 %collective-permute-start.9 = (bf16[2,320,128]{2,1,0:T(8,128)(2,1)S(1)}, bf16[2,320,128]{2,1,0:T(8,128)(2,1)S(1)}, u32[]{:S(2)}, u32[]{:S(2)}) collective-permute-start(bf16[2,320,128]{2,1,0:T(8,128)(2,1)S(1)} %get-tuple-element.28.own), channel_id=1, source_target_pairs={{0,496},{16,0},{32,16},{48,32},{64,48},{80,64},{96,80},{112,96},{1... | collective-permute-start | bytes 491528 | tf_op jit(solution)/shard_map/ppermute | solution.py:305
  62.5 6.0 %collective-permute-start.10 = (bf16[2,320,128]{2,1,0:T(8,128)(2,1)S(1)}, bf16[2,320,128]{2,1,0:T(8,128)(2,1)S(1)}, u32[]{:S(2)}, u32[]{:S(2)}) collective-permute-start(bf16[2,320,128]{2,1,0:T(8,128)(2,1)S(1)} %get-tuple-element.30.own), channel_id=1, source_target_pairs={{0,16},{16,32},{32,48},{48,64},{64,80},{80,96},{96,112},{112,128},... | collective-permute-start | bytes 491528 | tf_op jit(solution)/shard_map/ppermute | solution.py:305
  62.6 5.9 %collective-permute-start.11 = (bf16[2,320,128]{2,1,0:T(8,128)(2,1)S(1)}, bf16[2,320,128]{2,1,0:T(8,128)(2,1)S(1)}, u32[]{:S(2)}, u32[]{:S(2)}) collective-permute-start(bf16[2,320,128]{2,1,0:T(8,128)(2,1)S(1)} %get-tuple-element.30.own), channel_id=1, source_target_pairs={{0,496},{16,0},{32,16},{48,32},{64,48},{80,64},{96,80},{112,96},{1... | collective-permute-start | bytes 491528 | tf_op jit(solution)/shard_map/ppermute | solution.py:305
  69.3 6.0 %collective-permute-start.12 = (bf16[2,320,128]{2,1,0:T(8,128)(2,1)S(1)}, bf16[2,320,128]{2,1,0:T(8,128)(2,1)S(1)}, u32[]{:S(2)}, u32[]{:S(2)}) collective-permute-start(bf16[2,320,128]{2,1,0:T(8,128)(2,1)S(1)} %get-tuple-element.32.own), channel_id=1, source_target_pairs={{0,16},{16,32},{32,48},{48,64},{64,80},{80,96},{96,112},{112,128},... | collective-permute-start | bytes 491528 | tf_op jit(solution)/shard_map/ppermute | solution.py:305
  69.4 6.0 %collective-permute-start.13 = (bf16[2,320,128]{2,1,0:T(8,128)(2,1)S(1)}, bf16[2,320,128]{2,1,0:T(8,128)(2,1)S(1)}, u32[]{:S(2)}, u32[]{:S(2)}) collective-permute-start(bf16[2,320,128]{2,1,0:T(8,128)(2,1)S(1)} %get-tuple-element.32.own), channel_id=1, source_target_pairs={{0,496},{16,0},{32,16},{48,32},{64,48},{80,64},{96,80},{112,96},{1... | collective-permute-start | bytes 491528 | tf_op jit(solution)/shard_map/ppermute | solution.py:305

commit v4 on v3

--- a/solution.py
+++ b/solution.py
@@ -17,7 +17,8 @@
 SLOTS = 6
 MERGED = SLOTS * DOF
 TILES = MERGED // TILE
-HEAD = 2
+OWN = DOF // TILE
+HEAD = 5
 SPAN = 3
 LAST = DOF * FACES
 
@@ -73,11 +74,11 @@
 def put_own(columns, acc_ref):
     lane = lax.broadcasted_iota(jnp.int32, (DOF, TILE), 1)
     for tile in range(TILES):
-        if tile <= HEAD:
+        if tile <= OWN:
             acc_ref[tile] = columns(tile * TILE, (tile + 1) * TILE).astype(jnp.float32)
         else:
             acc_ref[tile] = jnp.zeros((DOF, TILE), jnp.float32)
-    acc_ref[HEAD] = jnp.where(lane < DOF - HEAD * TILE, acc_ref[HEAD], 0.0)
+    acc_ref[OWN] = jnp.where(lane < DOF - OWN * TILE, acc_ref[OWN], 0.0)
 
 
 def pick_kernel(departure, blocks, rhs, head, middle, last, row, sems):
@@ -90,7 +91,10 @@
     side.wait()
     head[:, RHS:] = row[:, 0 : HEAD * TILE]
     middle[...] = row[:, HEAD * TILE : LAST]
-    last[...] = row[:, LAST:]
+    for part in range(OWN):
+        last[part * DOF : (part + 1) * DOF] = row[:, LAST + part * TILE : LAST + (part + 1) * TILE]
+    rest = row[:, LAST + OWN * TILE :]
+    last[OWN * DOF :] = jnp.concatenate([rest[: DOF // 2], rest[DOF // 2 :]], axis=1)
 
 
 def pick(departure, blocks, rhs):
@@ -101,7 +105,7 @@
         out_shape=[
             vmem((DOF, RHS + HEAD * TILE), jnp.bfloat16),
             vmem((DOF, LAST - HEAD * TILE), jnp.bfloat16),
-            vmem((DOF, DOF), jnp.bfloat16),
+            vmem((DOF * DOF // TILE, TILE), jnp.bfloat16),
         ],
         scratch_shapes=[pltpu.VMEM((DOF, WIDE), jnp.bfloat16), pltpu.SemaphoreType.DMA((2,))],
         compiler_params=PARAMS,
@@ -223,6 +227,17 @@
         yield q, applied
 
 
+def last_moved(last, select):
+    whole = jnp.concatenate([last[part * DOF : (part + 1) * DOF] for part in range(OWN)], axis=1)
+    moved = jnp.dot(whole, select[: OWN * TILE], preferred_element_type=jnp.float32)
+    rest = last[OWN * DOF :]
+    edge = select[OWN * TILE :]
+    empty = jnp.zeros_like(edge)
+    upper = jnp.dot(rest, jnp.concatenate([edge, empty], axis=0), preferred_element_type=jnp.float32)
+    lower = jnp.dot(rest, jnp.concatenate([empty, edge], axis=0), preferred_element_type=jnp.float32)
+    return moved + jnp.concatenate([upper, lower], axis=0)
+
+
 def opening_kernel(
     arrival, neighbors, orientation, partial, acc, lo_last, hi_last, kept, own, below, above, merged, iterate, rounded
 ):
@@ -234,7 +249,7 @@
             def _():
                 face = FACES - 1
                 tile, select = turned_select(LAST, neighbors[0, 0, q, face], orientation[0, 0, q, face])
-                moved = jnp.dot(last[...], select, preferred_element_type=jnp.float32)
+                moved = last_moved(last, select)
                 for part in range(SPAN):
                     total = acc[q, tile + part] + moved[:, part * TILE : (part + 1) * TILE]
                     place = pl.multiple_of((tile + part) * TILE, TILE)
@@ -281,17 +296,22 @@
     )(*near(merged, kept, iterate, own, below, above))
 
 
-def closing_kernel(merged, kept, iterate, own, below, above, smoothed):
+def closing_kernel(merged, kept, iterate, own, below, above, smoothed, values, sems):
+    copies = [pltpu.make_async_copy(values.at[q], smoothed.at[0, 0, q], sems.at[q]) for q in range(KEPT)]
     for q, applied in applied_rows(merged, own, below, above):
-        smoothed[0, 0, q] = iterate[q] + RELAXATION * (kept[q].astype(jnp.float32) - applied)
+        values[q] = iterate[q] + RELAXATION * (kept[q].astype(jnp.float32) - applied)
+        copies[q].start()
+    for copy in copies:
+        copy.wait()
 
 
 def closing(merged, kept, iterate, own, below, above):
     return pl.pallas_call(
         closing_kernel,
         in_specs=[VMEM_SPEC] * 6,
-        out_specs=VMEM_SPEC,
+        out_specs=ANY_SPEC,
         out_shape=jax.ShapeDtypeStruct((1, 1, KEPT, DOF, RHS), jnp.float32),
+        scratch_shapes=[pltpu.VMEM((KEPT, DOF, RHS), jnp.float32), pltpu.SemaphoreType.DMA((KEPT,))],
         compiler_params=PARAMS,
         name="closing",
     )(*near(merged, kept, iterate, own, below, above))

time: 77.1 us -> 77.3 us (level)
  no operation moved by 1% of the time
where the time goes in v4:
time: 77.3 us; the launch traced here: 77 us
  starting transfers between devices  36.5 us (47%)
  waiting for transfers between devices  26.8 us (35%)
  Pallas kernels  13.3 us (17%)
    ppermute x14, starting transfers between devices, shifted(): return lax.ppermute(value, axis, pairs)  36.5 us
    ppermute x14, waiting for transfers between devices, shifted(): return lax.ppermute(value, axis, pairs)  26.8 us
    pallas_call x1, Pallas kernels, merged_local(): pl.pallas_call(local_kernel, in_specs=[SMEM_SPEC] * 3 + [ANY_SPEC], out_s...  3.41 us
    pallas_call x1, Pallas kernels, pick(): pl.pallas_call(pick_kernel, in_specs=[SMEM_SPEC] + [ANY_SPEC] * 2, out_sp...  2.38 us
    pallas_call x1, Pallas kernels, opening(): pl.pallas_call(opening_kernel, in_specs=[SMEM_SPEC] * 3 + [VMEM_SPEC] * 8...  1.95 us
    pallas_call x1, Pallas kernels, merged_arrived(): pl.pallas_call(arrived_kernel, in_specs=[SMEM_SPEC] * 3 + [VMEM_SPEC] * 5...  1.88 us
    pallas_call x2, Pallas kernels, middle(): pl.pallas_call(middle_kernel, in_specs=[VMEM_SPEC] * 6, out_specs=[VMEM_S...  1.59 us
  transfers between devices with their start and end apart: 14, of which 4 were waited for; matrix products, arithmetic and copies ran while one was open for 0% of the time, Pallas kernels for 8%

profile of v4, /device:TPU:6, one launch (start us, length us, event | category | flops | bytes accessed | tf_op | source)
XLA Modules:
  0.0 77.0 jit_solution(16162847558325892124)
XLA Ops:
  0.0 0.0 copy-start
  0.0 0.0 copy-start.3
  0.0 0.0 copy-start.1
  0.0 0.0 copy-start.2
  0.0 2.4 %pick.1 = (bf16[320,768]{1,0:T(8,128)(2,1)S(1)}, bf16[320,1280]{1,0:T(8,128)(2,1)S(1)}, bf16[800,128]{1,0:T(8,128)(2,1)S(1)}) custom-call(s32[1,1,2]{2,1,0:T(1,128)} %departure.1, bf16[1,1,3,320,2240]{4,3,2,1,0:T(8,128)(2,1)} %blocks.3, bf16[1,1,3,320,128]{4,3,2,1,0:T(8,128)(2,1)} %rhs.3), custom_call_target="tpu_custom_call" | custom-call | tf_op jit(solution)/shard_map/pick/pallas_call | solution.py:101
  2.4 3.5 %collective-permute-start.1 = (bf16[320,1280]{1,0:T(8,128)(2,1)S(1)}, bf16[320,1280]{1,0:T(8,128)(2,1)S(1)}, u32[]{:S(2)}, u32[]{:S(2)}) collective-permute-start(bf16[320,1280]{1,0:T(8,128)(2,1)S(1)} %get-tuple-element.20), channel_id=1, source_target_pairs={{0,1},{1,2},{2,3},{3,4},{4,5},{5,6},{6,7},{7,8},{8,9},{9,10},{10,1... | collective-permute-start | bytes 2457608 | tf_op jit(solution)/shard_map/ppermute | solution.py:325
  5.9 4.5 %collective-permute-start.3 = (bf16[320,1280]{1,0:T(8,128)(2,1)S(1)}, bf16[320,1280]{1,0:T(8,128)(2,1)S(1)}, u32[]{:S(2)}, u32[]{:S(2)}) collective-permute-start(bf16[320,1280]{1,0:T(8,128)(2,1)S(1)} %get-tuple-element.20), channel_id=1, source_target_pairs={{1,0},{2,1},{3,2},{4,3},{5,4},{6,5},{7,6},{8,7},{9,8},{10,9},{11,1... | collective-permute-start | bytes 2457608 | tf_op jit(solution)/shard_map/ppermute | solution.py:325
  10.4 1.9 %collective-permute-start = (bf16[320,768]{1,0:T(8,128)(2,1)S(1)}, bf16[320,768]{1,0:T(8,128)(2,1)S(1)}, u32[]{:S(2)}, u32[]{:S(2)}) collective-permute-start(bf16[320,768]{1,0:T(8,128)(2,1)S(1)} %get-tuple-element.19), channel_id=1, source_target_pairs={{0,1},{1,2},{2,3},{3,4},{4,5},{5,6},{6,7},{7,8},{8,9},{9,10},{10,1... | collective-permute-start | bytes 1474568 | tf_op jit(solution)/shard_map/ppermute | solution.py:325
  12.3 6.0 %collective-permute-start.2 = (bf16[320,768]{1,0:T(8,128)(2,1)S(1)}, bf16[320,768]{1,0:T(8,128)(2,1)S(1)}, u32[]{:S(2)}, u32[]{:S(2)}) collective-permute-start(bf16[320,768]{1,0:T(8,128)(2,1)S(1)} %get-tuple-element.19), channel_id=1, source_target_pairs={{1,0},{2,1},{3,2},{4,3},{5,4},{6,5},{7,6},{8,7},{9,8},{10,9},{11,1... | collective-permute-start | bytes 1474568 | tf_op jit(solution)/shard_map/ppermute | solution.py:325
  18.3 1.9 %collective-permute-start.4 = (bf16[800,128]{1,0:T(8,128)(2,1)S(1)}, bf16[800,128]{1,0:T(8,128)(2,1)S(1)}, u32[]{:S(2)}, u32[]{:S(2)}) collective-permute-start(bf16[800,128]{1,0:T(8,128)(2,1)S(1)} %get-tuple-element.23), channel_id=1, source_target_pairs={{0,1},{1,2},{2,3},{3,4},{4,5},{5,6},{6,7},{7,8},{8,9},{9,10},{10,1... | collective-permute-start | bytes 614408 | tf_op jit(solution)/shard_map/ppermute | solution.py:325
  20.3 17.8 %collective-permute-done.lo_head.lower = bf16[320,768]{1,0:T(8,128)(2,1)S(1)} collective-permute-done((bf16[320,768]{1,0:T(8,128)(2,1)S(1)}, bf16[320,768]{1,0:T(8,128)(2,1)S(1)}, u32[]{:S(2)}, u32[]{:S(2)}) %collective-permute-start) | collective-permute-done | bytes 491552 | tf_op jit(solution)/shard_map/ppermute | solution.py:325
  38.1 3.1 %collective-permute-start.5 = (bf16[800,128]{1,0:T(8,128)(2,1)S(1)}, bf16[800,128]{1,0:T(8,128)(2,1)S(1)}, u32[]{:S(2)}, u32[]{:S(2)}) collective-permute-start(bf16[800,128]{1,0:T(8,128)(2,1)S(1)} %get-tuple-element.23), channel_id=1, source_target_pairs={{1,0},{2,1},{3,2},{4,3},{5,4},{6,5},{7,6},{8,7},{9,8},{10,9},{11,1... | collective-permute-start | bytes 614408 | tf_op jit(solution)/shard_map/ppermute | solution.py:325
  41.1 0.0 collective-permute-done.2.hi_head.upper
  41.1 0.0 copy-done
  41.2 0.0 copy-done.3
  41.2 0.6 first.1
  41.8 0.0 collective-permute-start.6
  41.8 0.0 collective-permute-done.1.lo_middle
  41.8 6.7 %collective-permute-start.7 = (bf16[2,320,128]{2,1,0:T(8,128)(2,1)S(1)}, bf16[2,320,128]{2,1,0:T(8,128)(2,1)S(1)}, u32[]{:S(2)}, u32[]{:S(2)}) collective-permute-start(bf16[2,320,128]{2,1,0:T(8,128)(2,1)S(1)} %get-tuple-element.25.own), channel_id=1, source_target_pairs={{0,496},{16,0},{32,16},{48,32},{64,48},{80,64},{96,80},{112,96},{1... | collective-permute-start | bytes 491528 | tf_op jit(solution)/shard_map/ppermute | solution.py:325
  48.5 0.0 copy-done.1
  48.5 0.0 copy-done.2
  48.5 3.4 %merge_local.1.local = bf16[2,320,1920]{2,1,0:T(8,128)(2,1)S(1)} custom-call(s32[1,1,2]{2,1,0:T(1,128)S(1)} %copy-done.3, s32[1,1,2,6]{3,2,1,0:T(2,128)S(1)} %copy-done.1, s32[1,1,2,6]{3,2,1,0:T(2,128)S(1)} %copy-done.2, bf16[1,1,3,320,2240]{4,3,2,1,0:T(8,128)(2,1)} %blocks.3), custom_call_target="tpu_custom_call" | custom-call | tf_op jit(solution)/shard_map/merge_local/pallas_call | solution.py:169
  51.9 0.0 collective-permute-done.3.hi_middle
  51.9 1.9 %merge_arrived.1 = (bf16[2,320,1920]{2,1,0:T(8,128)(2,1)S(1)}, f32[2,15,320,128]{3,2,1,0:T(8,128)S(1)}) custom-call(s32[1,1,2]{2,1,0:T(1,128)S(1)} %copy-done.3, s32[1,1,2,6]{3,2,1,0:T(2,128)S(1)} %copy-done.1, s32[1,1,2,6]{3,2,1,0:T(2,128)S(1)} %copy-done.2, bf16[2,320,1920]{2,1,0:T(8,128)(2,1)S(1)} %merge_local.1.local, ...), custom_call_target="tpu_custom_call", output_to_operand_aliasing={{0}: (3, {})} | custom-call | tf_op jit(solution)/shard_map/merge_arrived/pallas_call | solution.py:207
  53.8 0.0 collective-permute-done.4.lo_last
  53.8 0.0 collective-permute-done.5.hi_last
  53.9 0.0 collective-permute-done.6.below
  53.9 0.0 collective-permute-done.7.above
  53.9 1.9 %opening.1 = (bf16[2,320,1920]{2,1,0:T(8,128)(2,1)S(1)}, f32[2,320,128]{2,1,0:T(8,128)S(1)}, bf16[2,320,128]{2,1,0:T(8,128)(2,1)S(1)}) custom-call(s32[1,1,2]{2,1,0:T(1,128)S(1)} %copy-done.3, s32[1,1,2,6]{3,2,1,0:T(2,128)S(1)} %copy-done.1, s32[1,1,2,6]{3,2,1,0:T(2,128)S(1)} %copy-done.2, ...), custom_call_target="tpu_custom_call", output_to_operand_aliasing={{0}: (3, {})} | custom-call | tf_op jit(solution)/shard_map/opening/pallas_call | solution.py:266
  55.8 0.0 collective-permute-start.8
  55.9 2.9 %collective-permute-start.9 = (bf16[2,320,128]{2,1,0:T(8,128)(2,1)S(1)}, bf16[2,320,128]{2,1,0:T(8,128)(2,1)S(1)}, u32[]{:S(2)}, u32[]{:S(2)}) collective-permute-start(bf16[2,320,128]{2,1,0:T(8,128)(2,1)S(1)} %get-tuple-element.28.own), channel_id=1, source_target_pairs={{0,496},{16,0},{32,16},{48,32},{64,48},{80,64},{96,80},{112,96},{1... | collective-permute-start | bytes 491528 | tf_op jit(solution)/shard_map/ppermute | solution.py:325
  58.8 3.0 %collective-permute-done.8.below = bf16[2,320,128]{2,1,0:T(8,128)(2,1)S(1)} collective-permute-done((bf16[2,320,128]{2,1,0:T(8,128)(2,1)S(1)}, bf16[2,320,128]{2,1,0:T(8,128)(2,1)S(1)}, u32[]{:S(2)}, u32[]{:S(2)}) %collective-permute-start.8) | collective-permute-done | bytes 163872 | tf_op jit(solution)/shard_map/ppermute | solution.py:325
  61.8 0.0 collective-permute-done.9.above
  61.8 0.8 %middle.2 = (f32[2,320,128]{2,1,0:T(8,128)S(1)}, bf16[2,320,128]{2,1,0:T(8,128)(2,1)S(1)}) custom-call(bf16[2,320,1920]{2,1,0:T(8,128)(2,1)S(1)} %get-tuple-element.26.merged, bf16[2,320,128]{2,1,0:T(8,128)(2,1)S(1)} %get-tuple-element.24.kept, f32[2,320,128]{2,1,0:T(8,128)S(1)} %get-tuple-element.27.iterate, ...), custom_call_target="tpu_custom_call" | custom-call | tf_op jit(solution)/shard_map/middle/pallas_call | solution.py:289
  62.6 0.0 collective-permute-start.10
  62.6 3.0 %collective-permute-start.11 = (bf16[2,320,128]{2,1,0:T(8,128)(2,1)S(1)}, bf16[2,320,128]{2,1,0:T(8,128)(2,1)S(1)}, u32[]{:S(2)}, u32[]{:S(2)}) collective-permute-start(bf16[2,320,128]{2,1,0:T(8,128)(2,1)S(1)} %get-tuple-element.30.own), channel_id=1, source_target_pairs={{0,496},{16,0},{32,16},{48,32},{64,48},{80,64},{96,80},{112,96},{1... | collective-permute-start | bytes 491528 | tf_op jit(solution)/shard_map/ppermute | solution.py:325
  65.6 3.0 %collective-permute-done.10.below = bf16[2,320,128]{2,1,0:T(8,128)(2,1)S(1)} collective-permute-done((bf16[2,320,128]{2,1,0:T(8,128)(2,1)S(1)}, bf16[2,320,128]{2,1,0:T(8,128)(2,1)S(1)}, u32[]{:S(2)}, u32[]{:S(2)}) %collective-permute-start.10) | collective-permute-done | bytes 163872 | tf_op jit(solution)/shard_map/ppermute | solution.py:325
  68.6 0.0 collective-permute-done.11.above
  68.6 0.8 %middle.3 = (f32[2,320,128]{2,1,0:T(8,128)S(1)}, bf16[2,320,128]{2,1,0:T(8,128)(2,1)S(1)}) custom-call(bf16[2,320,1920]{2,1,0:T(8,128)(2,1)S(1)} %get-tuple-element.26.merged, bf16[2,320,128]{2,1,0:T(8,128)(2,1)S(1)} %get-tuple-element.24.kept, f32[2,320,128]{2,1,0:T(8,128)S(1)} %get-tuple-element.29.iterate, ...), custom_call_target="tpu_custom_call" | custom-call | tf_op jit(solution)/shard_map/middle/pallas_call | solution.py:289
  69.4 0.0 collective-permute-start.12
  69.4 3.0 %collective-permute-start.13 = (bf16[2,320,128]{2,1,0:T(8,128)(2,1)S(1)}, bf16[2,320,128]{2,1,0:T(8,128)(2,1)S(1)}, u32[]{:S(2)}, u32[]{:S(2)}) collective-permute-start(bf16[2,320,128]{2,1,0:T(8,128)(2,1)S(1)} %get-tuple-element.32.own), channel_id=1, source_target_pairs={{0,496},{16,0},{32,16},{48,32},{64,48},{80,64},{96,80},{112,96},{1... | collective-permute-start | bytes 491528 | tf_op jit(solution)/shard_map/ppermute | solution.py:325
  72.4 3.0 %collective-permute-done.12.below = bf16[2,320,128]{2,1,0:T(8,128)(2,1)S(1)} collective-permute-done((bf16[2,320,128]{2,1,0:T(8,128)(2,1)S(1)}, bf16[2,320,128]{2,1,0:T(8,128)(2,1)S(1)}, u32[]{:S(2)}, u32[]{:S(2)}) %collective-permute-start.12) | collective-permute-done | bytes 163872 | tf_op jit(solution)/shard_map/ppermute | solution.py:325
  75.4 0.0 collective-permute-done.13.above
  75.4 1.5 %closing.1 = f32[1,1,2,320,128]{4,3,2,1,0:T(8,128)} custom-call(bf16[2,320,1920]{2,1,0:T(8,128)(2,1)S(1)} %get-tuple-element.26.merged, bf16[2,320,128]{2,1,0:T(8,128)(2,1)S(1)} %get-tuple-element.24.kept, f32[2,320,128]{2,1,0:T(8,128)S(1)} %get-tuple-element.31.iterate, bf16[2,320,128]{2,1,0:T(8,128)(2,1)S(1)} %get-tuple-element.32.own, ...), custom_call_target="tpu_custom_call" | custom-call | tf_op jit(solution)/shard_map/closing/pallas_call | solution.py:309
Async XLA Ops:
  0.0 41.1 %copy-start = (bf16[1,1,3,320,128]{4,3,2,1,0:T(8,128)(2,1)S(1)}, bf16[1,1,3,320,128]{4,3,2,1,0:T(8,128)(2,1)}, u32[]{:S(2)}) copy-start(bf16[1,1,3,320,128]{4,3,2,1,0:T(8,128)(2,1)} %rhs.3) | copy-start | bytes 737284
  0.0 41.2 %copy-start.3 = (s32[1,1,2]{2,1,0:T(1,128)S(1)}, s32[1,1,2]{2,1,0:T(1,128)}, u32[]{:S(2)}) copy-start(s32[1,1,2]{2,1,0:T(1,128)} %arrival.7) | copy-start | bytes 28
  0.0 48.5 %copy-start.1 = (s32[1,1,2,6]{3,2,1,0:T(2,128)S(1)}, s32[1,1,2,6]{3,2,1,0:T(2,128)}, u32[]{:S(2)}) copy-start(s32[1,1,2,6]{3,2,1,0:T(2,128)} %neighbors.5) | copy-start | bytes 148
  0.0 48.5 %copy-start.2 = (s32[1,1,2,6]{3,2,1,0:T(2,128)S(1)}, s32[1,1,2,6]{3,2,1,0:T(2,128)}, u32[]{:S(2)}) copy-start(s32[1,1,2,6]{3,2,1,0:T(2,128)} %orientation.5) | copy-start | bytes 148
  2.4 39.4 %collective-permute-start.1 = (bf16[320,1280]{1,0:T(8,128)(2,1)S(1)}, bf16[320,1280]{1,0:T(8,128)(2,1)S(1)}, u32[]{:S(2)}, u32[]{:S(2)}) collective-permute-start(bf16[320,1280]{1,0:T(8,128)(2,1)S(1)} %get-tuple-element.20), channel_id=1, source_target_pairs={{0,1},{1,2},{2,3},{3,4},{4,5},{5,6},{6,7},{7,8},{8,9},{9,10},{10,1... | collective-permute-start | bytes 2457608 | tf_op jit(solution)/shard_map/ppermute | solution.py:325
  5.9 46.0 %collective-permute-start.3 = (bf16[320,1280]{1,0:T(8,128)(2,1)S(1)}, bf16[320,1280]{1,0:T(8,128)(2,1)S(1)}, u32[]{:S(2)}, u32[]{:S(2)}) collective-permute-start(bf16[320,1280]{1,0:T(8,128)(2,1)S(1)} %get-tuple-element.20), channel_id=1, source_target_pairs={{1,0},{2,1},{3,2},{4,3},{5,4},{6,5},{7,6},{8,7},{9,8},{10,9},{11,1... | collective-permute-start | bytes 2457608 | tf_op jit(solution)/shard_map/ppermute | solution.py:325
  10.4 27.7 %collective-permute-start = (bf16[320,768]{1,0:T(8,128)(2,1)S(1)}, bf16[320,768]{1,0:T(8,128)(2,1)S(1)}, u32[]{:S(2)}, u32[]{:S(2)}) collective-permute-start(bf16[320,768]{1,0:T(8,128)(2,1)S(1)} %get-tuple-element.19), channel_id=1, source_target_pairs={{0,1},{1,2},{2,3},{3,4},{4,5},{5,6},{6,7},{7,8},{8,9},{9,10},{10,1... | collective-permute-start | bytes 1474568 | tf_op jit(solution)/shard_map/ppermute | solution.py:325
  12.3 28.8 %collective-permute-start.2 = (bf16[320,768]{1,0:T(8,128)(2,1)S(1)}, bf16[320,768]{1,0:T(8,128)(2,1)S(1)}, u32[]{:S(2)}, u32[]{:S(2)}) collective-permute-start(bf16[320,768]{1,0:T(8,128)(2,1)S(1)} %get-tuple-element.19), channel_id=1, source_target_pairs={{1,0},{2,1},{3,2},{4,3},{5,4},{6,5},{7,6},{8,7},{9,8},{10,9},{11,1... | collective-permute-start | bytes 1474568 | tf_op jit(solution)/shard_map/ppermute | solution.py:325
  18.3 35.5 %collective-permute-start.4 = (bf16[800,128]{1,0:T(8,128)(2,1)S(1)}, bf16[800,128]{1,0:T(8,128)(2,1)S(1)}, u32[]{:S(2)}, u32[]{:S(2)}) collective-permute-start(bf16[800,128]{1,0:T(8,128)(2,1)S(1)} %get-tuple-element.23), channel_id=1, source_target_pairs={{0,1},{1,2},{2,3},{3,4},{4,5},{5,6},{6,7},{7,8},{8,9},{9,10},{10,1... | collective-permute-start | bytes 614408 | tf_op jit(solution)/shard_map/ppermute | solution.py:325
  38.1 15.8 %collective-permute-start.5 = (bf16[800,128]{1,0:T(8,128)(2,1)S(1)}, bf16[800,128]{1,0:T(8,128)(2,1)S(1)}, u32[]{:S(2)}, u32[]{:S(2)}) collective-permute-start(bf16[800,128]{1,0:T(8,128)(2,1)S(1)} %get-tuple-element.23), channel_id=1, source_target_pairs={{1,0},{2,1},{3,2},{4,3},{5,4},{6,5},{7,6},{8,7},{9,8},{10,9},{11,1... | collective-permute-start | bytes 614408 | tf_op jit(solution)/shard_map/ppermute | solution.py:325
  41.8 12.1 %collective-permute-start.6 = (bf16[2,320,128]{2,1,0:T(8,128)(2,1)S(1)}, bf16[2,320,128]{2,1,0:T(8,128)(2,1)S(1)}, u32[]{:S(2)}, u32[]{:S(2)}) collective-permute-start(bf16[2,320,128]{2,1,0:T(8,128)(2,1)S(1)} %get-tuple-element.25.own), channel_id=1, source_target_pairs={{0,16},{16,32},{32,48},{48,64},{64,80},{80,96},{96,112},{112,128},... | collective-permute-start | bytes 491528 | tf_op jit(solution)/shard_map/ppermute | solution.py:325
  41.8 12.0 %collective-permute-start.7 = (bf16[2,320,128]{2,1,0:T(8,128)(2,1)S(1)}, bf16[2,320,128]{2,1,0:T(8,128)(2,1)S(1)}, u32[]{:S(2)}, u32[]{:S(2)}) collective-permute-start(bf16[2,320,128]{2,1,0:T(8,128)(2,1)S(1)} %get-tuple-element.25.own), channel_id=1, source_target_pairs={{0,496},{16,0},{32,16},{48,32},{64,48},{80,64},{96,80},{112,96},{1... | collective-permute-start | bytes 491528 | tf_op jit(solution)/shard_map/ppermute | solution.py:325
  55.8 6.0 %collective-permute-start.8 = (bf16[2,320,128]{2,1,0:T(8,128)(2,1)S(1)}, bf16[2,320,128]{2,1,0:T(8,128)(2,1)S(1)}, u32[]{:S(2)}, u32[]{:S(2)}) collective-permute-start(bf16[2,320,128]{2,1,0:T(8,128)(2,1)S(1)} %get-tuple-element.28.own), channel_id=1, source_target_pairs={{0,16},{16,32},{32,48},{48,64},{64,80},{80,96},{96,112},{112,128},... | collective-permute-start | bytes 491528 | tf_op jit(solution)/shard_map/ppermute | solution.py:325
  55.9 5.9 %collective-permute-start.9 = (bf16[2,320,128]{2,1,0:T(8,128)(2,1)S(1)}, bf16[2,320,128]{2,1,0:T(8,128)(2,1)S(1)}, u32[]{:S(2)}, u32[]{:S(2)}) collective-permute-start(bf16[2,320,128]{2,1,0:T(8,128)(2,1)S(1)} %get-tuple-element.28.own), channel_id=1, source_target_pairs={{0,496},{16,0},{32,16},{48,32},{64,48},{80,64},{96,80},{112,96},{1... | collective-permute-start | bytes 491528 | tf_op jit(solution)/shard_map/ppermute | solution.py:325
  62.6 6.0 %collective-permute-start.10 = (bf16[2,320,128]{2,1,0:T(8,128)(2,1)S(1)}, bf16[2,320,128]{2,1,0:T(8,128)(2,1)S(1)}, u32[]{:S(2)}, u32[]{:S(2)}) collective-permute-start(bf16[2,320,128]{2,1,0:T(8,128)(2,1)S(1)} %get-tuple-element.30.own), channel_id=1, source_target_pairs={{0,16},{16,32},{32,48},{48,64},{64,80},{80,96},{96,112},{112,128},... | collective-permute-start | bytes 491528 | tf_op jit(solution)/shard_map/ppermute | solution.py:325
  62.6 5.9 %collective-permute-start.11 = (bf16[2,320,128]{2,1,0:T(8,128)(2,1)S(1)}, bf16[2,320,128]{2,1,0:T(8,128)(2,1)S(1)}, u32[]{:S(2)}, u32[]{:S(2)}) collective-permute-start(bf16[2,320,128]{2,1,0:T(8,128)(2,1)S(1)} %get-tuple-element.30.own), channel_id=1, source_target_pairs={{0,496},{16,0},{32,16},{48,32},{64,48},{80,64},{96,80},{112,96},{1... | collective-permute-start | bytes 491528 | tf_op jit(solution)/shard_map/ppermute | solution.py:325
  69.4 6.0 %collective-permute-start.12 = (bf16[2,320,128]{2,1,0:T(8,128)(2,1)S(1)}, bf16[2,320,128]{2,1,0:T(8,128)(2,1)S(1)}, u32[]{:S(2)}, u32[]{:S(2)}) collective-permute-start(bf16[2,320,128]{2,1,0:T(8,128)(2,1)S(1)} %get-tuple-element.32.own), channel_id=1, source_target_pairs={{0,16},{16,32},{32,48},{48,64},{64,80},{80,96},{96,112},{112,128},... | collective-permute-start | bytes 491528 | tf_op jit(solution)/shard_map/ppermute | solution.py:325
  69.4 6.0 %collective-permute-start.13 = (bf16[2,320,128]{2,1,0:T(8,128)(2,1)S(1)}, bf16[2,320,128]{2,1,0:T(8,128)(2,1)S(1)}, u32[]{:S(2)}, u32[]{:S(2)}) collective-permute-start(bf16[2,320,128]{2,1,0:T(8,128)(2,1)S(1)} %get-tuple-element.32.own), channel_id=1, source_target_pairs={{0,496},{16,0},{32,16},{48,32},{64,48},{80,64},{96,80},{112,96},{1... | collective-permute-start | bytes 491528 | tf_op jit(solution)/shard_map/ppermute | solution.py:325
